TPU v7x, 16 devices: a 4x2x1 block of a 4x4x8 slice. The times are simulated.
16 devices in a mesh: rep: 4 (over y, z, core), dp: 4 (over x).
Axes of the slice: x: 4, y: 2, z: 1, core: 2. Of those that a mesh axis runs over, the one named last changes fastest.
The devices are a block of a 4x4x8 slice.
Arguments:
- x: bfloat16 [16, 4096, 512], P(('rep', 'dp')), parts along dimension 0
- dy: bfloat16 [16, 4096, 512], P(('rep', 'dp')), parts along dimension 0
- w_gate: bfloat16 [2, 512, 4096], replicated
- w_up: bfloat16 [2, 512, 4096], replicated
- w_down: bfloat16 [2, 4096, 512], replicated
- m_w_gate: float32 [2, 512, 4096], P(None, 'dp')
- m_w_up: float32 [2, 512, 4096], P(None, 'dp')
- m_w_down: float32 [2, 4096, 512], P(None, 'dp')
- v_w_gate: float32 [2, 512, 4096], P(None, 'dp')
- v_w_up: float32 [2, 512, 4096], P(None, 'dp')
- v_w_down: float32 [2, 4096, 512], P(None, 'dp')
Outputs:
- output 1: bfloat16 [8, 512, 4096], P('rep'), parts along dimension 0
- output 2: bfloat16 [8, 512, 4096], P('rep'), parts along dimension 0
- output 3: bfloat16 [8, 4096, 512], P('rep'), parts along dimension 0
- output 4: float32 [8, 512, 4096], P('rep', 'dp'), parts along dimension 0
- output 5: float32 [8, 512, 4096], P('rep', 'dp'), parts along dimension 0
- output 6: float32 [8, 4096, 512], P('rep', 'dp'), parts along dimension 0
- output 7: float32 [8, 512, 4096], P('rep', 'dp'), parts along dimension 0
- output 8: float32 [8, 512, 4096], P('rep', 'dp'), parts along dimension 0
- output 9: float32 [8, 4096, 512], P('rep', 'dp'), parts along dimension 0
There are 4 independent parts. A program takes and returns all parts, laid end to end along the dimension named above; an argument that names none is the same for every part.
All inputs are finite; a program needn't handle non-finite values.
Results may differ from a plain program's by a relative error of at most 0.022.
Values are sent between devices in bfloat16 or wider.
A program may use at most 768 MiB of HBM per device.

v0:
```python
import jax
import jax.numpy as jnp
from jax import lax

NAMES = ("w_gate", "w_up", "w_down")


def matmul(a, w):
    return jnp.dot(a, w, preferred_element_type=jnp.float32).astype(jnp.bfloat16)


def normed(h):
    wide = h.astype(jnp.float32)
    scale = lax.rsqrt(jnp.mean(wide**2, -1, keepdims=True) + 1e-6)
    return (wide * scale).astype(jnp.bfloat16)


def layer(h, w):
    a = normed(h)
    gate = jnp.dot(a, w["w_gate"], preferred_element_type=jnp.float32)
    up = jnp.dot(a, w["w_up"], preferred_element_type=jnp.float32)
    return h + matmul((jax.nn.silu(gate) * up).astype(jnp.bfloat16), w["w_down"])


def adamw(w, m, v, g):
    m = 0.9 * m + 0.1 * g
    v = 0.95 * v + 0.05 * g * g
    step = m * lax.rsqrt(v + 1e-8) + 0.1 * w
    return (w - 0.02 * step).astype(jnp.bfloat16), m, v


def stack(weights, h):
    for number in range(weights["w_gate"].shape[0]):
        h = layer(h, {name: w[number] for name, w in weights.items()})
    return h


def solution(mesh):
    groups = mesh.shape["rep"]

    def step(x, dy, *arrays):
        weights, m, v = (arrays[i : i + 3] for i in (0, 3, 6))
        x, dy = (t.reshape(groups, -1, *t.shape[1:]) for t in (x, dy))

        def of_a_group(x, dy):
            _, back = jax.vjp(lambda w: stack(w, x), dict(zip(NAMES, weights, strict=True)))
            by_weights = back(dy)[0]
            gradients = [by_weights[name].astype(jnp.float32) for name in NAMES]
            new = [adamw(w.astype(jnp.float32), m, v, g) for w, m, v, g in zip(weights, m, v, gradients, strict=True)]
            return tuple(one[which] for which in range(3) for one in new)

        return tuple(t.reshape(-1, *t.shape[2:]) for t in jax.vmap(of_a_group)(x, dy))

    return step
```

profile of v0, /device:TPU:112, one launch (start us, length us, event | category | flops | bytes accessed | tf_op | source)
XLA Modules:
  0.0 1153.8 jit_solution(745507805291894775)
XLA Ops:
  7.2 0.1 reduce-scatter.29.cloned.1.call-start
  7.3 3.1 fusion.35
  10.3 6.3 copy
  16.7 30.4 %fusion.104 = f32[4096,4096]{1,0:T(8,128)} fusion(bf16[2,512,4096]{2,1,0:T(8,128)(2,1)} %param, bf16[1,4096,512]{2,1,0:T(8,128)(2,1)} %param.2, f32[4096]{0:T(1024)S(1)} %add_rsqrt_fusion), kind=kOutput, calls=%fused_computation.124 | convolution fusion | flops 17186160640 | bytes 75513856 | tf_op jit(solution)/vmap(jvp())/dot_general | solution.py:20
  47.1 30.4 %fusion.102 = f32[4096,4096]{1,0:T(8,128)} fusion(bf16[2,512,4096]{2,1,0:T(8,128)(2,1)} %param.3, bf16[1,4096,512]{2,1,0:T(8,128)(2,1)} %param.2, f32[4096]{0:T(1024)S(1)} %add_rsqrt_fusion), kind=kOutput, calls=%fused_computation.122 | convolution fusion | flops 17186160640 | bytes 75513856 | tf_op jit(solution)/vmap(jvp())/dot_general | solution.py:21
  77.5 52.6 %fusion.26 = bf16[4096,4096]{1,0:T(8,128)(2,1)} fusion(f32[4096,4096]{1,0:T(8,128)} %fusion.102, f32[4096,4096]{1,0:T(8,128)} %fusion.104), kind=kLoop, calls=%fused_computation.35 | loop fusion | flops 100663296 | bytes 167772160
  130.1 24.7 %fusion.39 = (f32[4096]{0:T(1024)S(1)}, bf16[1,1,4096,512]{2,3,1,0:T(8,128)(2,1)}) fusion(bf16[4096,4096]{1,0:T(8,128)(2,1)} %fusion.26, bf16[2,4096,512]{2,1,0:T(8,128)(2,1)} %param.4, bf16[1,4096,512]{1,2,0:T(8,128)(2,1)} %copy), kind=kOutput, calls=%fused_computation.56 | convolution fusion | flops 17190350848 | bytes 46153728 | tf_op jit(solution)/vmap(jvp())/dot_general | solution.py:9
  154.9 0.6 copy-done.3
  155.5 30.2 %fusion.91 = f32[4096,4096]{1,0:T(8,128)} fusion(bf16[2,512,4096]{2,1,0:T(8,128)(2,1)} %param, bf16[1,1,4096,512]{2,3,1,0:T(8,128)(2,1)} %get-tuple-element.10, f32[4096]{0:T(1024)S(1)} %bitcast.427), kind=kOutput, calls=%fused_computation.111 | convolution fusion | flops 17186160640 | bytes 75513856 | tf_op jit(solution)/vmap(jvp())/dot_general | solution.py:20
  185.7 30.3 %fusion.94 = f32[4096,4096]{1,0:T(8,128)} fusion(bf16[2,512,4096]{2,1,0:T(8,128)(2,1)} %param.3, bf16[1,1,4096,512]{2,3,1,0:T(8,128)(2,1)} %get-tuple-element.10, f32[4096]{0:T(1024)S(1)} %bitcast.428), kind=kOutput, calls=%fused_computation.114 | convolution fusion | flops 17186160640 | bytes 75513856 | tf_op jit(solution)/vmap(jvp())/dot_general | solution.py:21
  216.0 24.8 %convolution_convert_fusion.1 = bf16[4096,4096]{1,0:T(8,128)(2,1)} fusion(bf16[1,4096,512]{2,1,0:T(8,128)(2,1)} %param.5, bf16[2,4096,512]{2,1,0:T(8,128)(2,1)} %param.4), kind=kOutput, calls=%fused_computation.44 | convolution fusion | flops 17196646400 | bytes 41943040 | tf_op jit(solution)/vmap(transpose(jvp()))/dot_general | solution.py:9
  240.9 6.3 copy.1
  247.2 62.9 %fusion.6 = bf16[4096,4096]{1,0:T(8,128)(2,1)} fusion(f32[4096,4096]{1,0:T(8,128)} %fusion.91, f32[4096,4096]{1,0:T(8,128)} %fusion.94, bf16[4096,4096]{1,0:T(8,128)(2,1)} %convolution_convert_fusion.1), kind=kLoop, calls=%fused_computation.11 | loop fusion | flops 201326592 | bytes 201326592
  310.1 23.8 %convolution_convert_fusion.2 = bf16[4096,512]{0,1:T(8,128)(2,1)} fusion(bf16[4096,4096]{1,0:T(8,128)(2,1)} %fusion.6, bf16[2,512,4096]{2,1,0:T(8,128)(2,1)} %param), kind=kOutput, calls=%fused_computation.70 | convolution fusion | flops 17179869184 | bytes 41943040 | tf_op jit(solution)/vmap(transpose(jvp()))/dot_general | solution.py:20
  333.9 39.3 %fusion.41 = (f32[4096]{0:T(1024)S(1)}, bf16[1,1,4096,512]{2,3,1,0:T(8,128)(2,1)}) fusion(bf16[1,1,4096,512]{2,3,1,0:T(8,128)(2,1)S(1)} %copy-done.2, bf16[4096,512]{0,1:T(8,128)(2,1)} %convolution_convert_fusion.2, bf16[2,512,4096]{2,1,0:T(8,128)(2,1)} %param.3, bf16[4096,4096]{1,0:T(8,128)(2,1)} %convolution_convert_fusion.1, f32[4096,4096]{1,0:T(8,128)} %fusion.91), kind=kOutput, calls=%fused_computation.58 | convolution fusion | flops 17293111296 | bytes 117456896 | tf_op jit(solution)/vmap(transpose(jvp()))/dot_general | solution.py:21
  373.2 0.1 multiply_multiply_fusion.3
  373.3 5.7 fusion.89
  378.9 26.1 %convolution_bitcast_fusion = f32[1,4096,512]{2,1,0:T(8,128)} fusion(bf16[4096,4096]{1,0:T(8,128)(2,1)} %fusion.26, bf16[4096,512]{0,1:T(8,128)(2,1)} %fusion.89), kind=kOutput, calls=%fused_computation.61 | convolution fusion | flops 17179869184 | bytes 46137344 | tf_op jit(solution)/vmap(transpose(jvp()))/dot_general | solution.py:9
  405.0 0.1 reduce-scatter.29.cloned.1.call-update
  405.1 0.1 reduce-scatter.27.cloned.1.call-start
  405.1 48.9 %fusion.42 = f32[1,4096,512]{2,1,0:T(8,128)} fusion(f32[4096,4096]{1,0:T(8,128)} %fusion.94, f32[4096,4096]{1,0:T(8,128)} %fusion.91, bf16[1,4096,512]{2,1,0:T(8,128)(2,1)} %param.5), kind=kOutput, calls=%fused_computation.60 | convolution fusion | flops 17280532480 | bytes 146800640 | tf_op jit(solution)/vmap(transpose(jvp()))/dot_general | solution.py:9
  454.0 0.1 reduce-scatter.27.cloned.1.call-update
  454.1 0.1 reduce-scatter.25.cloned.1.call-start
  454.2 24.6 %convolution_convert_fusion = bf16[4096,4096]{1,0:T(8,128)(2,1)} fusion(bf16[4096,512]{0,1:T(8,128)(2,1)} %fusion.89, bf16[2,4096,512]{2,1,0:T(8,128)(2,1)} %param.4), kind=kOutput, calls=%fused_computation.43 | convolution fusion | flops 17196646400 | bytes 41943040 | tf_op jit(solution)/vmap(transpose(jvp()))/dot_general | solution.py:9
  478.8 38.5 %fusion.51 = f32[1,512,4096]{2,1,0:T(8,128)} fusion(bf16[4096,4096]{1,0:T(8,128)(2,1)} %convolution_convert_fusion, f32[4096,4096]{1,0:T(8,128)} %fusion.104, bf16[1,4096,512]{1,2,0:T(8,128)(2,1)S(1)} %copy-done.1, f32[4096]{0:T(1024)S(1)} %copy-done.9), kind=kOutput, calls=%fused_computation.65 | convolution fusion | flops 17286823936 | bytes 113262592 | tf_op jit(solution)/vmap(transpose(jvp()))/dot_general | solution.py:21
  517.3 0.1 reduce-scatter.25.cloned.1.call-update
  517.3 0.1 reduce-scatter.23.cloned.1.call-start
  517.4 0.6 copy-done.7
  518.0 40.6 %fusion.45 = f32[1,512,4096]{2,1,0:T(8,128)} fusion(bf16[4096,4096]{1,0:T(8,128)(2,1)} %convolution_convert_fusion.1, f32[4096,4096]{1,0:T(8,128)} %fusion.91, bf16[1,1,4096,512]{2,3,1,0:T(8,128)(2,1)} %get-tuple-element.10, f32[4096]{0:T(1024)S(1)} %bitcast.430), kind=kOutput, calls=%fused_computation.63 | convolution fusion | flops 17286823936 | bytes 113262592 | tf_op jit(solution)/vmap(transpose(jvp()))/dot_general | solution.py:21
  558.6 0.1 reduce-scatter.23.cloned.1.call-update
  558.7 0.1 reduce-scatter.19.cloned.1.call-start
  558.8 24.1 %convolution_bitcast_fusion.1 = f32[1,512,4096]{2,1,0:T(8,128)} fusion(bf16[4096,4096]{1,0:T(8,128)(2,1)} %fusion.6, bf16[1,1,4096,512]{2,3,1,0:T(8,128)(2,1)} %get-tuple-element.10, f32[4096]{0:T(1024)S(1)} %bitcast.431), kind=kOutput, calls=%fused_computation.62 | convolution fusion | flops 17186160640 | bytes 46153728 | tf_op jit(solution)/vmap(transpose(jvp()))/dot_general | solution.py:20
  582.9 0.1 reduce-scatter.19.cloned.1.call-update
  583.0 0.1 reduce-scatter.21.cloned.1.call-start
  583.0 0.6 copy-done.10
  583.6 60.3 %fusion.48 = f32[1,512,4096]{2,1,0:T(8,128)} fusion(f32[4096,4096]{1,0:T(8,128)} %fusion.104, f32[4096,4096]{1,0:T(8,128)} %fusion.102, bf16[4096,4096]{1,0:T(8,128)(2,1)} %convolution_convert_fusion, bf16[1,4096,512]{1,2,0:T(8,128)(2,1)} %copy, f32[4096]{0:T(1024)S(1)} %copy-done.10), kind=kOutput, calls=%fused_computation.64 | convolution fusion | flops 17370710016 | bytes 180371456 | tf_op jit(solution)/vmap(transpose(jvp()))/dot_general | solution.py:20
  643.9 0.1 reduce-scatter.21.cloned.1.call-update
  644.0 0.1 all-gather.14.cloned.1.call-start
  644.1 0.5 copy-done.11
  644.6 0.6 dynamic-slice
  645.8 0.0 reduce-scatter.29.cloned.1.call-done
  645.9 1.7 convert_bitcast_fusion.3
  647.6 1.7 convert_bitcast_fusion.4
  649.3 7.7 fusion.124
  657.0 0.1 all-gather.14.cloned.1.call-update
  657.1 0.1 all-gather.12.cloned.1.call-start
  657.2 1.7 convert_bitcast_fusion.5
  658.9 61.8 %reduce-scatter.23.cloned.1.call-done = f32[1,128,4096]{2,1,0:T(8,128)} async-done(((f32[1,512,4096]{2,1,0:T(8,128)}), f32[1,128,4096]{2,1,0:T(8,128)}) %reduce-scatter.23.cloned.1.call-update) | async-done | bytes 2097168
  720.6 1.7 convert_bitcast_fusion.6
  722.4 7.6 fusion.125
  730.0 0.1 all-gather.12.cloned.1.call-update
  730.1 0.1 all-gather.10.cloned.1.call-start
  730.1 69.5 %reduce-scatter.19.cloned.1.call-done = f32[1,128,4096]{2,1,0:T(8,128)} async-done(((f32[1,512,4096]{2,1,0:T(8,128)}), f32[1,128,4096]{2,1,0:T(8,128)}) %reduce-scatter.19.cloned.1.call-update) | async-done | bytes 2097168
  799.6 1.7 convert_bitcast_fusion.8
  801.3 77.3 %reduce-scatter.21.cloned.1.call-done = f32[1,128,4096]{2,1,0:T(8,128)} async-done(((f32[1,512,4096]{2,1,0:T(8,128)}), f32[1,128,4096]{2,1,0:T(8,128)}) %reduce-scatter.21.cloned.1.call-update) | async-done | bytes 2097168
  878.6 1.7 convert_bitcast_fusion.7
  880.3 7.9 fusion.126
  888.2 0.1 all-gather.10.cloned.1.call-update
  888.2 70.8 %all-gather.14.cloned.1.call-done = bf16[1,2,4096,512]{3,2,1,0:T(8,128)(2,1)} async-done(((bf16[1,2,1024,512]{3,2,1,0:T(8,128)(2,1)}), bf16[1,2,4096,512]{3,2,1,0:T(8,128)(2,1)}) %all-gather.14.cloned.1.call-update) | async-done | bytes 8388624 | tf_op jit(solution)/reshape | solution.py:52
  959.1 82.3 %all-gather.12.cloned.1.call-done = bf16[1,2,512,4096]{3,2,1,0:T(8,128)(2,1)} async-done(((bf16[1,2,128,4096]{3,2,1,0:T(8,128)(2,1)}), bf16[1,2,512,4096]{3,2,1,0:T(8,128)(2,1)}) %all-gather.12.cloned.1.call-update) | async-done | bytes 8388624 | tf_op jit(solution)/reshape | solution.py:52
  1041.4 82.3 %all-gather.10.cloned.1.call-done = bf16[1,2,512,4096]{3,2,1,0:T(8,128)(2,1)} async-done(((bf16[1,2,128,4096]{3,2,1,0:T(8,128)(2,1)}), bf16[1,2,512,4096]{3,2,1,0:T(8,128)(2,1)}) %all-gather.10.cloned.1.call-update) | async-done | bytes 8388624 | tf_op jit(solution)/reshape | solution.py:52
  1123.7 7.9 copy.5
  1131.6 7.9 copy.6
  1139.5 7.3 copy.7
  (25 shorter events, 0.1 us)
Async XLA Ops:
  7.2 638.7 %reduce-scatter.29.cloned.1.call-start = ((), (), s32[]{:S(2)}) async-start(), calls=%async_computation.14 | async-start | bytes 10485760
  16.7 30.5 %copy-start.8 = (f32[4096]{0:T(1024)}, f32[4096]{0:T(1024)S(1)}, u32[]{:S(2)}) copy-start(f32[4096]{0:T(1024)S(1)} %add_rsqrt_fusion) | copy-start | bytes 49156
  154.8 0.6 copy-start.3
  155.5 30.2 %copy-start.5 = (f32[1,1,4096]{2,1,0:T(1,128)}, f32[1,1,4096]{2,1,0:T(1,128)S(1)}, u32[]{:S(2)}) copy-start(f32[1,1,4096]{2,1,0:T(1,128)S(1)} %rsqrt.31) | copy-start | bytes 49156
  310.1 23.8 %copy-start.2 = (bf16[1,1,4096,512]{2,3,1,0:T(8,128)(2,1)S(1)}, bf16[1,1,4096,512]{2,3,1,0:T(8,128)(2,1)}, u32[]{:S(2)}) copy-start(bf16[1,1,4096,512]{2,3,1,0:T(8,128)(2,1)} %get-tuple-element.10) | copy-start | bytes 12582916
  333.9 39.3 %copy-start.4 = (f32[4096]{0:T(1024)S(1)}, f32[4096]{0:T(1024)}, u32[]{:S(2)}) copy-start(f32[4096]{0:T(1024)} %copy-done.3) | copy-start | bytes 49156
  333.9 39.4 %copy-start = (bf16[1,4096,512]{1,2,0:T(8,128)(2,1)S(1)}, bf16[1,4096,512]{1,2,0:T(8,128)(2,1)}, u32[]{:S(2)}) copy-start(bf16[1,4096,512]{1,2,0:T(8,128)(2,1)} %copy.1) | copy-start | bytes 12582916
  333.9 39.4 %copy-start.6 = (f32[1,1,4096]{2,1,0:T(1,128)S(1)}, f32[1,1,4096]{2,1,0:T(1,128)}, u32[]{:S(2)}) copy-start(f32[1,1,4096]{2,1,0:T(1,128)} %copy-done.5) | copy-start | bytes 49156
  405.1 242.5 %reduce-scatter.27.cloned.1.call-start = ((), (), s32[]{:S(2)}) async-start(), calls=%async_computation.13 | async-start | bytes 10485760
  454.1 24.7 %copy-start.9 = (f32[4096]{0:T(1024)S(1)}, f32[4096]{0:T(1024)}, u32[]{:S(2)}) copy-start(f32[4096]{0:T(1024)} %copy-done.8) | copy-start | bytes 49156
  454.1 203.1 %reduce-scatter.25.cloned.1.call-start = ((), (), s32[]{:S(2)}) async-start(), calls=%async_computation.12 | async-start | bytes 10485760
  454.2 24.6 %copy-start.1 = (bf16[1,4096,512]{1,2,0:T(8,128)(2,1)S(1)}, bf16[1,4096,512]{1,2,0:T(8,128)(2,1)}, u32[]{:S(2)}) copy-start(bf16[1,4096,512]{1,2,0:T(8,128)(2,1)} %copy) | copy-start | bytes 12582916
  517.3 0.7 copy-start.7
  517.3 203.3 %reduce-scatter.23.cloned.1.call-start = ((), (), s32[]{:S(2)}) async-start(), calls=%async_computation.11 | async-start | bytes 10485760
  558.7 240.9 %reduce-scatter.19.cloned.1.call-start = ((), (), s32[]{:S(2)}) async-start(), calls=%async_computation.9 | async-start | bytes 10485760
  582.9 0.7 copy-start.10
  583.0 295.6 %reduce-scatter.21.cloned.1.call-start = ((), (), s32[]{:S(2)}) async-start(), calls=%async_computation.10 | async-start | bytes 10485760
  643.9 0.7 copy-start.11
  644.0 315.1 %all-gather.14.cloned.1.call-start = ((), (), s32[]{:S(2)}) async-start(), calls=%async_computation.8 | async-start | bytes 10485760 | tf_op jit(solution)/reshape | solution.py:52
  657.1 384.3 %all-gather.12.cloned.1.call-start = ((), (), s32[]{:S(2)}) async-start(), calls=%async_computation.7 | async-start | bytes 10485760 | tf_op jit(solution)/reshape | solution.py:52
  730.1 393.6 %all-gather.10.cloned.1.call-start = ((), (), s32[]{:S(2)}) async-start(), calls=%async_computation.6 | async-start | bytes 10485760 | tf_op jit(solution)/reshape | solution.py:52
Sparse Core Ops, SparseCore 0:
  405.2 79.3 reduce-scatter.28
  486.9 76.1 reduce-scatter.26
  566.0 76.1 reduce-scatter.24
  644.4 76.1 reduce-scatter.22
  723.4 76.1 reduce-scatter.18
  802.4 76.1 reduce-scatter.20
  880.1 78.9 all-gather.13
  961.2 80.1 all-gather.11
  1043.5 80.1 all-gather.9
where the time goes:
time: 1160 us; the launch traced here: 1150 us
  matrix products  497 us (43%)
  waiting for transfers between devices  444 us (38%)
  other arithmetic  158 us (14%)
  local copies, waits for them, and re-layouts  38.7 us (3%)
  between operations  15.1 us (1%)
    reshape x3, waiting for transfers between devices, step(): t.reshape(-1, *t.shape[2:])  235 us
    unnamed x15, waiting for transfers between devices  209 us
    dot_general x5, matrix products, layer(): up = jnp.dot(a, w['w_up'], preferred_element_type=jnp.float32)  179 us
    dot_general x5, matrix products, layer(): gate = jnp.dot(a, w['w_gate'], preferred_element_type=jnp.float32)  169 us
    dot_general x5, matrix products, matmul(): jnp.dot(a, w, preferred_element_type=jnp.float32).astype(jnp.bfloat16)  149 us
    unnamed x3, other arithmetic  121 us
    unnamed x29, local copies, waits for them, and re-layouts  38.1 us
    reshape x3, other arithmetic, step(): t.reshape(-1, *t.shape[2:])  23.2 us
  transfers between devices with their start and end apart: 9, of which 6 were waited for; matrix products, arithmetic and copies ran while one was open for 23% of the time, Pallas kernels for 0%

commit v1 on v0

v1 whole, which is shorter than its diff:
```python
import functools

import jax
import jax.numpy as jnp
from jax import lax
from jax.experimental import pallas as pl
from jax.experimental.pallas import tpu as pltpu
from jax.sharding import PartitionSpec as P

F32, BF16 = jnp.float32, jnp.bfloat16
NN = (((1,), (0,)), ((), ()))
NT = (((1,), (1,)), ((), ()))
LANES = 128
CHUNKS = 2


def dot(a, b, dims):
    return lax.dot_general(a, b, dims, preferred_element_type=F32)


def normed(h):
    wide = h.astype(F32)
    return (wide * lax.rsqrt(jnp.mean(wide * wide, -1, keepdims=True) + 1e-6)).astype(BF16)


def forward_body(part, x_ref, wg_ref, wu_ref, wd_ref, a_ref, h_ref, b_ref, acc):
    x = x_ref[...]
    a = normed(x)
    a_ref[...] = a
    for k in range(wg_ref.shape[1] // part):
        s = slice(k * part, (k + 1) * part)
        gate, up = dot(a, wg_ref[:, s], NN), dot(a, wu_ref[:, s], NN)
        act = (gate * jax.nn.sigmoid(gate) * up).astype(BF16)
        term = dot(act, wd_ref[s, :], NN)
        acc[...] = term if k == 0 else acc[...] + term
    h = x + acc[...].astype(BF16)
    h_ref[...] = h
    b_ref[...] = normed(h)


def forward(x, wg, wu, wd, layer, tile=512, part=512):
    tokens, d = x.shape
    ff = wg.shape[2]
    rows = pl.BlockSpec((tile, d), lambda t: (t, 0))
    whole = lambda a, b: pl.BlockSpec((None, a, b), lambda t: (layer, 0, 0), pipeline_mode=pl.Buffered(1))
    return pl.pallas_call(
        functools.partial(forward_body, part),
        grid=(tokens // tile,),
        in_specs=[rows, whole(d, ff), whole(d, ff), whole(ff, d)],
        out_specs=[rows] * 3,
        out_shape=[jax.ShapeDtypeStruct((tokens, d), BF16)] * 3,
        scratch_shapes=[pltpu.VMEM((tile, d), F32)],
        compiler_params=pltpu.CompilerParams(dimension_semantics=("arbitrary",), vmem_limit_bytes=60 * 2**20),
        cost_estimate=pl.CostEstimate(flops=6 * tokens * d * ff, bytes_accessed=8 * tokens * d + 6 * d * ff, transcendentals=0),
        name="forward",
    )(x, wg, wu, wd)


def backward_body(n, part, need, first, *refs):
    refs = list(refs)
    a_ref, dy_ref = refs[:2]
    wg, wu, wd_ref = refs[2 : 2 + n], refs[2 + n : 2 + 2 * n], refs[2 + 2 * n]
    refs = refs[3 + 2 * n :]
    if need and not first:
        da_in = refs.pop(0)
    if need == 2:
        h_ref = refs.pop(0)
    out = refs.pop(0)
    if need:
        da_out = refs.pop(0)
    wg_t, wu_t, wg_c, wu_c, sum_g, sum_u, sum_d = refs
    t, last = pl.program_id(0), pl.num_programs(0) - 1
    w, d = wg[0].shape[1], a_ref.shape[1]
    units = n * w

    @pl.when(t == 0)
    def _():
        for j in range(n):
            s = slice(j * w, (j + 1) * w)
            for source, turned, plain in ((wg[j], wg_t, wg_c), (wu[j], wu_t, wu_c)):
                value = source[...]
                turned[s, :] = value.T
                if need:
                    plain[:, s] = value
        for total in (sum_g, sum_u, sum_d):
            total[...] = jnp.zeros_like(total)

    a, dy = a_ref[...], dy_ref[...]
    wd = wd_ref[...].reshape(units, d)
    da = None
    for k in range(units // part):
        s = slice(k * part, (k + 1) * part)
        gate, up = dot(wg_t[s, :], a, NT), dot(wu_t[s, :], a, NT)
        d_act = dot(wd[s, :], dy, NT).astype(BF16).astype(F32)
        sig = jax.nn.sigmoid(gate)
        silu = gate * sig
        act = (silu * up).astype(BF16)
        d_up = (d_act * silu).astype(BF16)
        d_gate = (d_act * up * (sig + silu * (1.0 - sig))).astype(BF16)
        sum_d[s, :] += dot(act, dy, NN)
        sum_g[s, :] += dot(d_gate, a, NN)
        sum_u[s, :] += dot(d_up, a, NN)
        if need:
            term = dot(wg_c[:, s], d_gate, NN) + dot(wu_c[:, s], d_up, NN)
            da = term if da is None else da + term
    if need:
        if not first:
            da = da + da_in[...]
        if need == 1:
            da_out[...] = da
        else:
            d_a = da.T.astype(BF16).astype(F32)
            h = h_ref[...].astype(F32)
            scale = lax.rsqrt(jnp.mean(h * h, -1, keepdims=True) + 1e-6)
            d_h = d_a * scale - h * (scale * scale * scale * jnp.mean(d_a * h, -1, keepdims=True))
            da_out[...] = dy + d_h.astype(BF16)

    @pl.when(t == last)
    def _():
        for o in range(n):
            lanes = slice(o * LANES, (o + 1) * LANES)
            out[o, 0:units, :] = sum_g[:, lanes].astype(BF16)
            out[o, units : 2 * units, :] = sum_u[:, lanes].astype(BF16)
            for i in range(d // LANES):
                out[o, 2 * units + i * w : 2 * units + (i + 1) * w, :] = sum_d[o * w : (o + 1) * w, i * LANES : (i + 1) * LANES].astype(BF16)


def backward(n, chunk, layer, a, dy, wg, wu, wd, da, h, need, tile=512, part=512):
    tokens, d = a.shape
    ff = wg.shape[2]
    w = ff // n // CHUNKS
    units = n * w
    first = da is None
    rows, columns = pl.BlockSpec((tile, d), lambda t: (t, 0)), pl.BlockSpec((d, tile), lambda t: (0, t))
    once = pl.Buffered(1)
    column = lambda j: pl.BlockSpec((None, d, w), lambda t: (layer, 0, j * CHUNKS + chunk), pipeline_mode=once)
    ins = [a, dy] + [wg] * n + [wu] * n + [wd.reshape(wd.shape[0], n, ff // n, d)]
    specs = [rows, rows] + [column(j) for j in range(n)] * 2
    specs.append(pl.BlockSpec((None, n, w, d), lambda t: (layer, 0, chunk, 0), pipeline_mode=once))
    outs = [jax.ShapeDtypeStruct((n, 3 * units, LANES), BF16)]
    out_specs = [pl.BlockSpec(outs[0].shape, lambda t: (0, 0, 0), pipeline_mode=once)]
    aliases = {}
    if need and not first:
        if need == 1:
            aliases = {len(ins): 1}
        ins.append(da)
        specs.append(columns)
    if need == 2:
        ins.append(h)
        specs.append(rows)
        outs.append(jax.ShapeDtypeStruct((tokens, d), BF16))
        out_specs.append(rows)
    if need == 1:
        outs.append(jax.ShapeDtypeStruct((d, tokens), F32))
        out_specs.append(columns)
    return pl.pallas_call(
        functools.partial(backward_body, n, part, need, first),
        grid=(tokens // tile,),
        in_specs=specs,
        out_specs=out_specs,
        out_shape=outs,
        scratch_shapes=[pltpu.VMEM((units, d), BF16)] * 2 + [pltpu.VMEM((d, units), BF16)] * 2 + [pltpu.VMEM((units, d), F32)] * 3,
        input_output_aliases=aliases,
        compiler_params=pltpu.CompilerParams(dimension_semantics=("arbitrary",), vmem_limit_bytes=60 * 2**20),
        cost_estimate=pl.CostEstimate(flops=(12 + 4 * bool(need)) * tokens * d * units, bytes_accessed=30 * tokens * d, transcendentals=0),
        name="backward",
    )(*ins)


def adamw(w, m, v, g):
    m = 0.9 * m + 0.1 * g
    v = 0.95 * v + 0.05 * g * g
    step = m * lax.rsqrt(v + 1e-8) + 0.1 * w
    return (w - 0.02 * step).astype(BF16), m, v


def solution(mesh):
    n = mesh.shape["dp"]

    def step(x, dy, wg, wu, wd, *moments):
        layers, d, ff = wg.shape
        w = ff // n // CHUNKS
        units = n * w
        me = lax.axis_index("dp")
        ms, vs = moments[:3], moments[3:]
        inputs, states = [], [x[0]]
        for layer in range(layers - 1):
            a, h, b = forward(states[-1], wg, wu, wd, layer)
            inputs.append(a)
            states.append(h)
        inputs.append(b)
        chunks = {}
        dh = dy[0]
        for layer in reversed(range(layers)):
            da = None
            for chunk in range(CHUNKS):
                need = 0 if layer == 0 else 1 + (chunk == CHUNKS - 1)
                grads, *rest = backward(n, chunk, layer, inputs[layer], dh, wg, wu, wd, da, states[layer], need)
                da = rest[0] if rest else None
                total = lax.psum_scatter(grads, "dp", scatter_dimension=0, tiled=True)[0].astype(F32)
                g = [total[i * units : (i + 1) * units].T.reshape(d // n, n, w) for i in range(2)]
                g.append(jnp.moveaxis(total[2 * units :].reshape(d // LANES, w, LANES), 0, 1).reshape(w, d))
                pick = lambda t: t.reshape(d // n, n, CHUNKS, w)[:, :, chunk]
                cut = lambda i, t: pick(t[layer]) if i < 2 else t[layer].reshape(CHUNKS, w, d)[chunk]
                own = [
                    lax.dynamic_slice(t[layer], (me * (d // n), 0), (d // n, ff)) if i < 2 else lax.dynamic_slice(t[layer], (me * (ff // n), 0), (ff // n, d))
                    for i, t in enumerate((wg, wu, wd))
                ]
                own = [pick(t) if i < 2 else t.reshape(CHUNKS, w, d)[chunk] for i, t in enumerate(own)]
                new = [adamw(own[i].astype(F32), cut(i, ms[i]), cut(i, vs[i]), g[i]) for i in range(3)]
                sent = jnp.concatenate([new[i][0].reshape(-1, d) for i in range(3)])
                everyone = lax.all_gather(sent, "dp", axis=0)
                chunks[layer, chunk] = new, everyone
            dh = da
        outs = []
        for i in range(3):
            rows = (3 * units * LANES) // 3 // d
            parts = [[chunks[layer, c][1][:, i * rows : (i + 1) * rows] for c in range(CHUNKS)] for layer in range(layers)]
            if i < 2:
                whole = [jnp.stack([p.reshape(n, d // n, n, w) for p in ps], 3).reshape(d, ff) for ps in parts]
            else:
                whole = [jnp.stack(ps, 1).reshape(ff, d) for ps in parts]
            outs.append(jnp.stack(whole))
        for which in (1, 2):
            for i in range(3):
                parts = [[chunks[layer, c][0][i][which] for c in range(CHUNKS)] for layer in range(layers)]
                if i < 2:
                    whole = [jnp.stack(ps, 2).reshape(d // n, ff) for ps in parts]
                else:
                    whole = [jnp.concatenate(ps) for ps in parts]
                outs.append(jnp.stack(whole))
        return tuple(outs)

    batch, split = P(("rep", "dp"), None, None), P(None, "dp", None)
    return jax.shard_map(
        step,
        mesh=mesh,
        in_specs=(batch, batch) + (P(),) * 3 + (split,) * 6,
        out_specs=(P("rep", None, None),) * 3 + (P("rep", "dp", None),) * 6,
        check_vma=False,
    )
```

time: 1160 us -> 1110 us (0.957)
  matrix products: 497 us -> 0 us
  local copies, waits for them, and re-layouts: 38.7 us -> 477 us
  waiting for transfers between devices: 444 us -> 68.7 us
  Pallas kernels: 0 us -> 375 us
    dot_general x15 -> x0, matrix products: 497 us -> none  [the longest x5 179 us: layer(): up = jnp.dot(a, w['w_up'], preferred_element_type=jnp.float32)]
    pallas_call x0 -> x5, Pallas kernels: none -> 375 us  [the longest x4 314 us: backward(): pl.pallas_call(functools.partial(backward_body, n, part, need, first), gr...]
    reshape x3 -> x0, waiting for transfers between devices: 235 us -> none  [step(): t.reshape(-1, *t.shape[2:])]
    another operation x1 -> x42, local copies, waits for them, and re-layouts: 0.58 us -> 219 us  [the longest x8 88.6 us: step(): jnp.stack([p.reshape(n, d // n, n, w) for p in ps], 3).reshape(d, ff)]
    unnamed x15 -> x8, waiting for transfers between devices: 209 us -> 1.6 us
    unnamed x3 -> x0, other arithmetic: 121 us -> none
    another operation x0 -> x21, other arithmetic: none -> 99.8 us  [the longest x4 43.7 us: step(): jnp.stack([p.reshape(n, d // n, n, w) for p in ps], 3).reshape(d, ff)]
    reduce_scatter x0 -> x4, waiting for transfers between devices: none -> 67.1 us  [step(): lax.psum_scatter(grads, 'dp', scatter_dimension=0, tiled=True)[0]]
  transfers between devices with their start and end apart: 9 -> 8, of which waited for: 6 -> 2; matrix products, arithmetic and copies ran while one was open for 23% -> 38% of each run, Pallas kernels for 0% -> 6%
where the time goes in v1:
time: 1110 us; the launch traced here: 1100 us
  local copies, waits for them, and re-layouts  477 us (43%)
  Pallas kernels  375 us (34%)
  other arithmetic  159 us (14%)
  waiting for transfers between devices  68.7 us (6%)
  between operations  15.1 us (1%)
    pallas_call x4, Pallas kernels, backward(): pl.pallas_call(functools.partial(backward_body, n, part, need, first), gr...  314 us
    another operation x8, local copies, waits for them, and re-layouts, step(): jnp.stack([p.reshape(n, d // n, n, w) for p in ps], 3).reshape(d, ff)  88.6 us
    reduce_scatter x4, waiting for transfers between devices, step(): lax.psum_scatter(grads, 'dp', scatter_dimension=0, tiled=True)[0]  67.1 us
    unnamed x166, local copies, waits for them, and re-layouts  65.4 us
    pallas_call x1, Pallas kernels, forward(): pl.pallas_call(functools.partial(forward_body, part), grid=(tokens // til...  61.1 us
    another operation x12, local copies, waits for them, and re-layouts, step(): outs.append(jnp.stack(whole))  54.3 us
    another operation x4, other arithmetic, step(): jnp.stack([p.reshape(n, d // n, n, w) for p in ps], 3).reshape(d, ff)  43.7 us
    another operation x11, other arithmetic, step(): outs.append(jnp.stack(whole))  39.2 us
  transfers between devices with their start and end apart: 8, of which 2 were waited for; matrix products, arithmetic and copies ran while one was open for 38% of the time, Pallas kernels for 6%

profile of v1, /device:TPU:112, one launch (start us, length us, event | category | flops | bytes accessed | tf_op | source)
XLA Modules:
  0.0 1095.3 jit_solution(2969800587746717570)
XLA Ops:
  7.3 61.1 %forward.1 = (bf16[4096,512]{1,0:T(8,128)(2,1)}, bf16[4096,512]{1,0:T(8,128)(2,1)}, bf16[4096,512]{1,0:T(8,128)(2,1)}) custom-call(bf16[4096,512]{1,0:T(8,128)(2,1)} %bitcast.239, bf16[2,512,4096]{2,1,0:T(8,128)(2,1)} %refs_5_.7, bf16[2,512,4096]{2,1,0:T(8,128)(2,1)} %refs_9_.7, bf16[2,4096,512]{2,1,0:T(8,128)(2,1)} %wd_ref.1), custom_call_target="tpu_custom_call" | custom-call | flops 51539607552 | bytes 29360128 | tf_op jit(solution)/shard_map/forward/pallas_call | solution.py:46
  68.4 86.5 %backward.4 = (bf16[4,6144,128]{2,1,0:T(8,128)(2,1)}, f32[512,4096]{1,0:T(8,128)}) custom-call(bf16[4096,512]{1,0:T(8,128)(2,1)} %get-tuple-element.17.refs_0_, bf16[4096,512]{1,0:T(8,128)(2,1)} %bitcast.240, bf16[2,512,4096]{2,1,0:T(8,128)(2,1)} %refs_5_.7, bf16[2,512,4096]{2,1,0:T(8,128)(2,1)} %refs_5_.7, bf16[2,512,4096]{2,1,0:T(8,128)(2,1)} %refs_5_.7, ...), custom_call_target="tpu_custom_call" | custom-call | flops 68719476736 | bytes 62914560 | tf_op jit(solution)/shard_map/backward/pallas_call | solution.py:156
  154.9 89.2 %backward.5 = (bf16[4,6144,128]{2,1,0:T(8,128)(2,1)}, bf16[4096,512]{1,0:T(8,128)(2,1)}) custom-call(bf16[4096,512]{1,0:T(8,128)(2,1)} %get-tuple-element.17.refs_0_, bf16[4096,512]{1,0:T(8,128)(2,1)} %bitcast.241, bf16[2,512,4096]{2,1,0:T(8,128)(2,1)} %refs_5_.7, bf16[2,512,4096]{2,1,0:T(8,128)(2,1)} %refs_5_.7, bf16[2,512,4096]{2,1,0:T(8,128)(2,1)} %refs_5_.7, ...), custom_call_target="tpu_custom_call" | custom-call | flops 68719476736 | bytes 62914560 | tf_op jit(solution)/shard_map/backward/pallas_call | solution.py:156
  244.1 69.4 %backward.6 = bf16[4,6144,128]{2,1,0:T(8,128)(2,1)} custom-call(bf16[4096,512]{1,0:T(8,128)(2,1)} %get-tuple-element.16.refs_0_, bf16[4096,512]{1,0:T(8,128)(2,1)} %get-tuple-element.20.refs_1_, bf16[2,512,4096]{2,1,0:T(8,128)(2,1)} %refs_5_.7, bf16[2,512,4096]{2,1,0:T(8,128)(2,1)} %refs_5_.7, bf16[2,512,4096]{2,1,0:T(8,128)(2,1)} %refs_5_.7, ...), custom_call_target="tpu_custom_call" | custom-call | flops 51539607552 | bytes 62914560 | tf_op jit(solution)/shard_map/backward/pallas_call | solution.py:156
  313.6 69.1 %backward.7 = bf16[4,6144,128]{2,1,0:T(8,128)(2,1)} custom-call(bf16[4096,512]{1,0:T(8,128)(2,1)} %get-tuple-element.16.refs_0_, bf16[4096,512]{1,0:T(8,128)(2,1)} %get-tuple-element.20.refs_1_, bf16[2,512,4096]{2,1,0:T(8,128)(2,1)} %refs_5_.7, bf16[2,512,4096]{2,1,0:T(8,128)(2,1)} %refs_5_.7, bf16[2,512,4096]{2,1,0:T(8,128)(2,1)} %refs_5_.7, ...), custom_call_target="tpu_custom_call" | custom-call | flops 51539607552 | bytes 62914560 | tf_op jit(solution)/shard_map/backward/pallas_call | solution.py:156
  384.3 4.8 fusion.103
  391.4 3.2 reshape_squeeze.16
  406.8 4.0 fusion.100
  414.5 4.7 fusion.105
  425.2 3.6 copy.226
  428.8 4.7 fusion.106
  433.5 3.4 reshape_squeeze.19
  439.9 3.6 copy.227
  443.5 4.0 fusion.101
  452.4 5.8 fusion.102
  481.0 3.7 fusion.84
  492.7 3.4 fusion.19
  500.3 7.9 reduce-scatter.11.cloned.1.call-done
  511.4 59.2 %reduce-scatter.9.cloned.1.call-done = bf16[1,6144,128]{2,1,0:T(8,128)(2,1)} async-done(((bf16[4,6144,128]{2,1,0:T(8,128)(2,1)}), bf16[1,6144,128]{2,1,0:T(8,128)(2,1)}) %reduce-scatter.9.cloned.1.call-update) | async-done | bytes 1572880 | tf_op jit(solution)/shard_map/reduce_scatter | solution.py:200
  574.2 6.3 fusion.2
  584.4 3.6 copy.229
  592.1 3.6 copy.230
  595.7 3.6 copy.231
  603.2 3.4 fusion.81
  622.9 3.7 fusion.85
  640.0 3.2 reshape_squeeze.20
  646.2 3.6 copy.240
  655.8 3.6 copy.241
  670.6 3.4 reshape_squeeze.23
  677.0 3.6 copy.243
  689.5 3.7 fusion.83
  710.6 3.7 fusion.87
  732.3 3.8 copy.234
  736.1 3.6 copy.235
  743.6 3.6 copy.238
  747.2 3.7 copy.239
  754.8 3.4 fusion.82
  788.7 3.5 pad_maximum_fusion.17
  798.0 4.2 pad_maximum_fusion.18
  808.2 4.2 pad_maximum_fusion.15
  818.2 4.2 pad_maximum_fusion.16
  875.3 5.4 slice_bitcast_fusion.3
  880.7 5.4 slice_bitcast_fusion.2
  889.0 5.7 slice_bitcast_fusion
  894.7 5.4 slice_bitcast_fusion.1
  902.9 12.7 %stack_reshape.92 = bf16[4,128,4,1,512]{4,3,2,1,0:T(2,128)(2,1)} reshape(bf16[4,512,512]{2,1,0:T(8,128)(2,1)} %get-tuple-element.54) | data formatting | bytes 4194304 | tf_op jit(solution)/shard_map/stack;reshape | solution.py:220
  915.6 12.7 %stack_reshape.93 = bf16[4,128,4,1,512]{4,3,2,1,0:T(2,128)(2,1)} reshape(bf16[4,512,512]{2,1,0:T(8,128)(2,1)} %get-tuple-element.57) | data formatting | bytes 4194304 | tf_op jit(solution)/shard_map/stack;reshape | solution.py:220
  928.3 10.9 pad_maximum_fusion.5
  939.2 7.8 stack_reshape.74
  947.0 12.7 %stack_reshape.95 = bf16[4,128,4,1,512]{4,3,2,1,0:T(2,128)(2,1)} reshape(bf16[4,512,512]{2,1,0:T(8,128)(2,1)} %get-tuple-element.63) | data formatting | bytes 4194304 | tf_op jit(solution)/shard_map/stack;reshape | solution.py:220
  959.7 12.7 %stack_reshape.94 = bf16[4,128,4,1,512]{4,3,2,1,0:T(2,128)(2,1)} reshape(bf16[4,512,512]{2,1,0:T(8,128)(2,1)} %get-tuple-element.60) | data formatting | bytes 4194304 | tf_op jit(solution)/shard_map/stack;reshape | solution.py:220
  972.4 10.9 pad_maximum_fusion.6
  983.3 7.8 stack_reshape.77
  991.0 6.2 stack_reshape.88
  997.3 12.7 %stack_reshape.89 = bf16[4,128,4,1,512]{4,3,2,1,0:T(2,128)(2,1)} reshape(bf16[4,512,512]{2,1,0:T(8,128)(2,1)} %get-tuple-element.58) | data formatting | bytes 4194304 | tf_op jit(solution)/shard_map/stack;reshape | solution.py:220
  1010.0 11.0 %pad_maximum_fusion.3 = bf16[4,128,4,2,512]{4,3,2,1,0:T(2,128)(2,1)} fusion(bf16[4,128,4,1,512]{4,3,2,1,0:T(2,128)(2,1)} %stack_reshape.89, bf16[4,128,4,1,512]{4,3,2,1,0:T(2,128)(2,1)} %stack_reshape.88), kind=kLoop, calls=%fused_computation.3 | loop fusion | flops 8388608 | bytes 8388608 | tf_op jit(solution)/shard_map/stack | solution.py:220
  1021.0 7.9 stack_reshape.68
  1028.9 6.2 stack_reshape.91
  1035.1 12.7 %stack_reshape.90 = bf16[4,128,4,1,512]{4,3,2,1,0:T(2,128)(2,1)} reshape(bf16[4,512,512]{2,1,0:T(8,128)(2,1)} %get-tuple-element.61) | data formatting | bytes 4194304 | tf_op jit(solution)/shard_map/stack;reshape | solution.py:220
  1047.8 10.9 pad_maximum_fusion.4
  1058.7 7.8 stack_reshape.71
  1066.5 7.8 pad_maximum_fusion.2
  1074.3 6.3 pad_maximum_fusion.1
  1080.6 7.6 pad_maximum_fusion
  (312 shorter events, 298.3 us)
Async XLA Ops:
  7.2 451.1 %reduce-scatter.5.cloned.1.call-start = ((), (), s32[]{:S(2)}) async-start(), calls=%async_computation.4 | async-start | bytes 7864320 | tf_op jit(solution)/shard_map/reduce_scatter | solution.py:200
  313.6 183.8 %reduce-scatter.7.cloned.1.call-start = ((), (), s32[]{:S(2)}) async-start(), calls=%async_computation.5 | async-start | bytes 7864320 | tf_op jit(solution)/shard_map/reduce_scatter | solution.py:200
  382.7 125.4 %reduce-scatter.11.cloned.1.call-start = ((), (), s32[]{:S(2)}) async-start(), calls=%async_computation.7 | async-start | bytes 7864320 | tf_op jit(solution)/shard_map/reduce_scatter | solution.py:200
  383.5 187.0 %reduce-scatter.9.cloned.1.call-start = ((), (), s32[]{:S(2)}) async-start(), calls=%async_computation.6 | async-start | bytes 7864320 | tf_op jit(solution)/shard_map/reduce_scatter | solution.py:200
  384.2 491.1 %all-gather.9.cloned.1.call-start = ((), (), s32[]{:S(2)}) async-start(), calls=%async_computation.8 | async-start | bytes 7864320 | tf_op jit(solution)/shard_map/all_gather | solution.py:212
  384.2 4.9 copy-start.35
  458.2 3.1 copy-start.21
  458.2 3.1 copy-start.22
  466.2 7.9 copy-start.4
  475.8 5.2 copy-start.23
  475.8 5.2 copy-start.24
  484.7 3.2 copy-start.32
  489.7 2.9 copy-start.38
  492.6 3.4 copy-start.39
  492.6 3.4 copy-start.45
  492.6 3.4 copy-start.49
  492.7 3.4 copy-start.53
  511.4 62.2 %copy-start.36 = (f32[1,2048,128]{2,1,0:T(8,128)S(1)}, f32[1,2048,128]{2,1,0:T(8,128)}, u32[]{:S(2)}) copy-start(f32[1,2048,128]{2,1,0:T(8,128)} %get-tuple-element.99) | copy-start | bytes 3145732
  570.5 3.0 copy-start.16
  570.5 3.7 copy-start.37
  574.2 6.3 copy-start.71
  574.2 6.3 copy-start.72
  581.8 6.2 copy-start.18
  581.9 298.8 %all-gather.11.cloned.1.call-start = ((), (), s32[]{:S(2)}) async-start(), calls=%async_computation.9 | async-start | bytes 7864320 | tf_op jit(solution)/shard_map/all_gather | solution.py:212
  589.4 10.0 copy-start.19
  608.1 7.9 copy-start.3
  617.7 5.2 copy-start.27
  617.7 5.2 copy-start.29
  626.6 3.2 copy-start.33
  631.6 2.9 copy-start.40
  634.5 2.8 copy-start.50
  634.5 3.1 copy-start.54
  640.0 249.0 %all-gather.15.cloned.1.call-start = ((), (), s32[]{:S(2)}) async-start(), calls=%async_computation.11 | async-start | bytes 7864320 | tf_op jit(solution)/shard_map/all_gather | solution.py:212
  674.1 6.5 copy-start.17
  681.9 7.6 copy-start.25
  695.9 7.9 copy-start.2
  705.4 5.2 copy-start.26
  714.4 5.3 copy-start.34
  726.4 2.9 copy-start.43
  726.4 2.9 copy-start.47
  726.4 3.1 copy-start.51
  726.4 3.4 copy-start.55
  732.1 7.6 copy-start.20
  732.2 162.5 %all-gather.13.cloned.1.call-start = ((), (), s32[]{:S(2)}) async-start(), calls=%async_computation.10 | async-start | bytes 7864320 | tf_op jit(solution)/shard_map/all_gather | solution.py:212
  747.2 7.6 copy-start.31
  760.9 6.6 copy-start.1
  769.1 3.0 copy-start.28
  769.1 3.0 copy-start.30
  778.7 4.2 copy-start.41
  781.6 3.9 copy-start.44
  795.2 2.8 copy-start.67
  805.2 3.0 copy-start.57
  815.4 2.8 copy-start.66
  848.4 3.2 copy-start.62
  853.9 3.0 copy-start.60
  853.9 3.7 copy-start.61
  858.0 3.7 copy-start.7
  861.8 3.7 copy-start.9
  865.5 3.7 copy-start.11
  869.2 3.7 copy-start.13
  880.7 5.4 copy-start.14
  894.7 5.4 copy-start.15
  1021.0 7.9 copy-start.5
  1066.5 7.8 copy-start
  (17 other events, 37.5 us)
Sparse Core Ops, SparseCore 0:
  313.7 62.7 reduce-scatter.4
  382.9 62.7 reduce-scatter.6
  448.6 59.5 reduce-scatter.10
  510.9 59.5 reduce-scatter.8
  582.0 61.2 all-gather.8
  644.7 62.2 all-gather.10
  732.3 61.2 all-gather.14
  795.2 62.2 all-gather.12

commit v2 on v1

--- a/solution.py
+++ b/solution.py
@@ -7,11 +7,13 @@
 from jax.experimental.pallas import tpu as pltpu
 from jax.sharding import PartitionSpec as P
 
+
 F32, BF16 = jnp.float32, jnp.bfloat16
 NN = (((1,), (0,)), ((), ()))
 NT = (((1,), (1,)), ((), ()))
 LANES = 128
-CHUNKS = 2
+HALF = 2
+LAST, EARLIER = ((8, 0), (8, 1), (4, 1), (4, 2), (4, 3)), ((4, 0), (4, 1), (4, 2), (4, 3))
 
 
 def dot(a, b, dims):
@@ -21,6 +23,10 @@
 def normed(h):
     wide = h.astype(F32)
     return (wide * lax.rsqrt(jnp.mean(wide * wide, -1, keepdims=True) + 1e-6)).astype(BF16)
+
+
+def sigmoid(t):
+    return 0.5 * jnp.tanh(0.5 * t) + 0.5
 
 
 def forward_body(part, x_ref, wg_ref, wu_ref, wd_ref, a_ref, h_ref, b_ref, acc):
@@ -30,7 +36,7 @@
     for k in range(wg_ref.shape[1] // part):
         s = slice(k * part, (k + 1) * part)
         gate, up = dot(a, wg_ref[:, s], NN), dot(a, wu_ref[:, s], NN)
-        act = (gate * jax.nn.sigmoid(gate) * up).astype(BF16)
+        act = (gate * sigmoid(gate) * up).astype(BF16)
         term = dot(act, wd_ref[s, :], NN)
         acc[...] = term if k == 0 else acc[...] + term
     h = x + acc[...].astype(BF16)
@@ -56,8 +62,8 @@
     )(x, wg, wu, wd)
 
 
-def backward_body(n, part, need, first, *refs):
-    refs = list(refs)
+def backward_body(n, part, need, first, waits, *refs):
+    refs = list(refs)[waits:]
     a_ref, dy_ref = refs[:2]
     wg, wu, wd_ref = refs[2 : 2 + n], refs[2 + n : 2 + 2 * n], refs[2 + 2 * n]
     refs = refs[3 + 2 * n :]
@@ -92,7 +98,7 @@
         s = slice(k * part, (k + 1) * part)
         gate, up = dot(wg_t[s, :], a, NT), dot(wu_t[s, :], a, NT)
         d_act = dot(wd[s, :], dy, NT).astype(BF16).astype(F32)
-        sig = jax.nn.sigmoid(gate)
+        sig = sigmoid(gate)
         silu = gate * sig
         act = (silu * up).astype(BF16)
         d_up = (d_act * silu).astype(BF16)
@@ -125,17 +131,18 @@
                 out[o, 2 * units + i * w : 2 * units + (i + 1) * w, :] = sum_d[o * w : (o + 1) * w, i * LANES : (i + 1) * LANES].astype(BF16)
 
 
-def backward(n, chunk, layer, a, dy, wg, wu, wd, da, h, need, tile=512, part=512):
+def backward(n, share, layer, a, dy, wg, wu, wd, da, h, need, after, tile=512, part=512):
     tokens, d = a.shape
     ff = wg.shape[2]
-    w = ff // n // CHUNKS
+    pieces, chunk = share
+    w = ff // n // pieces
     units = n * w
     first = da is None
     rows, columns = pl.BlockSpec((tile, d), lambda t: (t, 0)), pl.BlockSpec((d, tile), lambda t: (0, t))
     once = pl.Buffered(1)
-    column = lambda j: pl.BlockSpec((None, d, w), lambda t: (layer, 0, j * CHUNKS + chunk), pipeline_mode=once)
-    ins = [a, dy] + [wg] * n + [wu] * n + [wd.reshape(wd.shape[0], n, ff // n, d)]
-    specs = [rows, rows] + [column(j) for j in range(n)] * 2
+    column = lambda j: pl.BlockSpec((None, d, w), lambda t: (layer, 0, j * pieces + chunk), pipeline_mode=once)
+    ins = list(after) + [a, dy] + [wg] * n + [wu] * n + [wd.reshape(wd.shape[0], n, ff // n, d)]
+    specs = [pl.BlockSpec(memory_space=pl.ANY)] * len(after) + [rows, rows] + [column(j) for j in range(n)] * 2
     specs.append(pl.BlockSpec((None, n, w, d), lambda t: (layer, 0, chunk, 0), pipeline_mode=once))
     outs = [jax.ShapeDtypeStruct((n, 3 * units, LANES), BF16)]
     out_specs = [pl.BlockSpec(outs[0].shape, lambda t: (0, 0, 0), pipeline_mode=once)]
@@ -154,7 +161,7 @@
         outs.append(jax.ShapeDtypeStruct((d, tokens), F32))
         out_specs.append(columns)
     return pl.pallas_call(
-        functools.partial(backward_body, n, part, need, first),
+        functools.partial(backward_body, n, part, need, first, len(after)),
         grid=(tokens // tile,),
         in_specs=specs,
         out_specs=out_specs,
@@ -174,14 +181,97 @@
     return (w - 0.02 * step).astype(BF16), m, v
 
 
+def update_body(kept, waits, me_ref, *refs):
+    g, w, m, v = (refs[3 * i : 3 * i + 3] for i in range(4))
+    sent, *new = refs[12 + kept + waits :]
+    for i in range(3):
+        grad = g[i][...].astype(F32)
+        if i < 2:
+            grad = grad.T
+        one, new[i][...], new[3 + i][...] = adamw(w[i][...].astype(F32), m[i][...], v[i][...], grad)
+        if i < 2:
+            sent[i] = one
+        else:
+            for q in range(one.shape[0] // LANES):
+                sent[i, :, q * LANES : (q + 1) * LANES] = one[q * LANES : (q + 1) * LANES]
+
+
+def update(me, n, share, layer, total, weights, ms, vs, done, after):
+    pieces, chunk = share
+    _, _, ff = weights[0].shape
+    w = ff // n // pieces
+    grad = [pl.BlockSpec((w, LANES), functools.partial(lambda i, j, me: (i * n + j, 0), i)) for i in range(3)]
+    across = pl.BlockSpec((None, LANES, w), lambda j, me: (layer, 0, j * pieces + chunk))
+    down = pl.BlockSpec((None, w, LANES), lambda j, me: (layer, chunk, j))
+    own = pl.BlockSpec((None, LANES, w), lambda j, me: (layer, me[0], j * pieces + chunk))
+    own_down = pl.BlockSpec((None, w, LANES), lambda j, me: (layer, me[0] * pieces + chunk, j))
+    moments = [across, across, down] * 2
+    ins = [total] * 3 + list(weights) + list(ms) + list(vs) + list(done) + list(after)
+    specs = grad + [own, own, own_down] + moments + [pl.BlockSpec(memory_space=pl.ANY)] * (len(done) + len(after))
+    return pl.pallas_call(
+        functools.partial(update_body, len(done), len(after)),
+        grid_spec=pltpu.PrefetchScalarGridSpec(
+            num_scalar_prefetch=1,
+            grid=(n,),
+            in_specs=specs,
+            out_specs=[pl.BlockSpec((None, 3, LANES, w), lambda j, me: (j, 0, 0, 0))] + moments,
+        ),
+        out_shape=[jax.ShapeDtypeStruct((n, 3, LANES, w), BF16)] + [jax.ShapeDtypeStruct(t.shape, F32) for t in (*ms, *vs)],
+        input_output_aliases={13 + i: 1 + i for i in range(len(done))},
+        compiler_params=pltpu.CompilerParams(dimension_semantics=("arbitrary",)),
+        cost_estimate=pl.CostEstimate(flops=8 * 10**9, bytes_accessed=60 * LANES * n * w, transcendentals=0),
+        name="update",
+    )(me, *ins)
+
+
+def place_body(n, pieces, chunk, layer, kept, me_ref, own, right, left, far_a, far_b, *refs):
+    outs, done = refs[kept : kept + 3], refs[-1]
+    w, near = own.shape[3], n // HALF
+    copies = []
+    for r in range(n):
+        owner = lax.rem(me_ref[0] + r, n)
+        rows = pl.ds(pl.multiple_of(owner * LANES, LANES), LANES)
+        for j in range(n):
+            ref, at = {0: (own, j), 1: (right, j), n - 1: (left, j)}.get(r, (far_a, j) if j < near else (far_b, j - near))
+            columns = pl.ds((j * pieces + chunk) * w, w)
+            copies += [(ref.at[at, i], outs[i].at[layer, rows, columns]) for i in range(2)]
+            for q in range(w // LANES):
+                part = pl.ds(pl.multiple_of((owner * pieces + chunk) * w + q * LANES, LANES), LANES)
+                copies.append((ref.at[at, 2, :, q * LANES : (q + 1) * LANES], outs[2].at[layer, part, j * LANES : (j + 1) * LANES]))
+    copies = [pltpu.make_async_copy(a, b, done.at[i]) for i, (a, b) in enumerate(copies)]
+    for copy in copies:
+        copy.start()
+    for copy in copies:
+        copy.wait()
+
+
+def place(me, n, share, layer, blocks, weights, done):
+    pieces, chunk = share
+    _, d, ff = weights[0].shape
+    w = ff // n // pieces
+    here, anywhere = pl.BlockSpec(memory_space=pltpu.VMEM), pl.BlockSpec(memory_space=pl.ANY)
+    return pl.pallas_call(
+        functools.partial(place_body, n, pieces, chunk, layer, len(done)),
+        in_specs=[pl.BlockSpec(memory_space=pltpu.SMEM)] + [here] * len(blocks) + [anywhere] * len(done),
+        out_specs=[anywhere] * 3,
+        out_shape=[jax.ShapeDtypeStruct(t.shape, BF16) for t in weights],
+        scratch_shapes=[pltpu.SemaphoreType.DMA((n * n * (2 + w // LANES),))],
+        input_output_aliases={1 + len(blocks) + i: i for i in range(len(done))},
+        cost_estimate=pl.CostEstimate(flops=4 * 10**9, bytes_accessed=12 * d * w, transcendentals=0),
+        name="place",
+    )(me, *blocks, *done)
+
+
 def solution(mesh):
     n = mesh.shape["dp"]
-
-    def step(x, dy, wg, wu, wd, *moments):
-        layers, d, ff = wg.shape
-        w = ff // n // CHUNKS
-        units = n * w
-        me = lax.axis_index("dp")
+    to_right = [(i, (i + 1) % n) for i in range(n)]
+    to_left = [(i, (i - 1) % n) for i in range(n)]
+
+    def work(x, dy, wg, wu, wd, *moments):
+        layers, d, _ = wg.shape
+        assert d == n * LANES and n == 2 * HALF
+        weights = (wg, wu, wd)
+        me = lax.axis_index("dp")[None].astype(jnp.int32)
         ms, vs = moments[:3], moments[3:]
         inputs, states = [], [x[0]]
         for layer in range(layers - 1):
@@ -189,51 +279,60 @@
             inputs.append(a)
             states.append(h)
         inputs.append(b)
-        chunks = {}
-        dh = dy[0]
-        for layer in reversed(range(layers)):
-            da = None
-            for chunk in range(CHUNKS):
-                need = 0 if layer == 0 else 1 + (chunk == CHUNKS - 1)
-                grads, *rest = backward(n, chunk, layer, inputs[layer], dh, wg, wu, wd, da, states[layer], need)
-                da = rest[0] if rest else None
-                total = lax.psum_scatter(grads, "dp", scatter_dimension=0, tiled=True)[0].astype(F32)
-                g = [total[i * units : (i + 1) * units].T.reshape(d // n, n, w) for i in range(2)]
-                g.append(jnp.moveaxis(total[2 * units :].reshape(d // LANES, w, LANES), 0, 1).reshape(w, d))
-                pick = lambda t: t.reshape(d // n, n, CHUNKS, w)[:, :, chunk]
-                cut = lambda i, t: pick(t[layer]) if i < 2 else t[layer].reshape(CHUNKS, w, d)[chunk]
-                own = [
-                    lax.dynamic_slice(t[layer], (me * (d // n), 0), (d // n, ff)) if i < 2 else lax.dynamic_slice(t[layer], (me * (ff // n), 0), (ff // n, d))
-                    for i, t in enumerate((wg, wu, wd))
-                ]
-                own = [pick(t) if i < 2 else t.reshape(CHUNKS, w, d)[chunk] for i, t in enumerate(own)]
-                new = [adamw(own[i].astype(F32), cut(i, ms[i]), cut(i, vs[i]), g[i]) for i in range(3)]
-                sent = jnp.concatenate([new[i][0].reshape(-1, d) for i in range(3)])
-                everyone = lax.all_gather(sent, "dp", axis=0)
-                chunks[layer, chunk] = new, everyone
-            dh = da
-        outs = []
-        for i in range(3):
-            rows = (3 * units * LANES) // 3 // d
-            parts = [[chunks[layer, c][1][:, i * rows : (i + 1) * rows] for c in range(CHUNKS)] for layer in range(layers)]
-            if i < 2:
-                whole = [jnp.stack([p.reshape(n, d // n, n, w) for p in ps], 3).reshape(d, ff) for ps in parts]
-            else:
-                whole = [jnp.stack(ps, 1).reshape(ff, d) for ps in parts]
-            outs.append(jnp.stack(whole))
-        for which in (1, 2):
-            for i in range(3):
-                parts = [[chunks[layer, c][0][i][which] for c in range(CHUNKS)] for layer in range(layers)]
-                if i < 2:
-                    whole = [jnp.stack(ps, 2).reshape(d // n, ff) for ps in parts]
-                else:
-                    whole = [jnp.concatenate(ps) for ps in parts]
-                outs.append(jnp.stack(whole))
-        return tuple(outs)
+        shares = [(layer, s) for layer in reversed(range(layers)) for s in (LAST if layer == layers - 1 else EARLIER)]
+        count = len(shares)
+        total, sent, near, new, placed = {}, {}, {}, (), ()
+
+        def send(t, pairs):
+            return lax.ppermute(t, "dp", pairs)
+
+        def renew(i, new, after):
+            layer, share = shares[i]
+            sent[i], *new = update(me, n, share, layer, total[i], weights, ms, vs, new, after)
+            near[i] = [send(sent[i], p) for p in (to_right, to_left)]
+            return new
+
+        def relay(i):
+            half = n // HALF
+            first = near[i][0][:half], near[i][1][half:]
+            near[i] += [send(first[j], p) for j, p in enumerate((to_right, to_left))]
+            return list(first)
+
+        def settle(i, placed):
+            layer, share = shares[i]
+            from_left, from_right, far_a, far_b = near[i]
+            return place(me, n, share, layer, [sent[i], from_right, from_left, far_a, far_b], weights, placed)
+
+        dh, da = dy[0], None
+        for k, (layer, share) in enumerate(shares):
+            after = []
+            if k >= 2:
+                new = renew(k - 2, new, [])
+                after.append(sent[k - 2])
+            if k >= 3:
+                after += relay(k - 3)
+            if k >= 4:
+                placed = settle(k - 4, placed)
+                after.append(placed[0])
+            final = k + 1 == count or shares[k + 1][0] != layer
+            need = 0 if layer == 0 else 1 + final
+            grads, *rest = backward(n, share, layer, inputs[layer], dh, wg, wu, wd, da, states[layer], need, after)
+            da = rest[0] if rest else None
+            total[k] = lax.psum_scatter(grads, "dp", scatter_dimension=0, tiled=True)[0]
+            if final:
+                dh, da = da, None
+        for i in (count - 2, count - 1):
+            after = relay(i - 1)
+            placed = settle(i - 2, placed)
+            new = renew(i, new, after + [placed[0]])
+        relay(count - 1)
+        for i in (count - 2, count - 1):
+            placed = settle(i, placed)
+        return (*placed, *new)
 
     batch, split = P(("rep", "dp"), None, None), P(None, "dp", None)
     return jax.shard_map(
-        step,
+        work,
         mesh=mesh,
         in_specs=(batch, batch) + (P(),) * 3 + (split,) * 6,
         out_specs=(P("rep", None, None),) * 3 + (P("rep", "dp", None),) * 6,

time: 1110 us -> 796 us (0.72)
  the two profiles are of different devices: /device:TPU:112 before, /device:TPU:120 now
where the time goes in v2:
time: 796 us; the launch traced here: 786 us
  Pallas kernels  464 us (58%)
  waiting for transfers between devices  221 us (28%)
  starting transfers between devices  64.6 us (8%)
  local copies, waits for them, and re-layouts  20.7 us (3%)
  between operations  15 us (2%)
    pallas_call x9, Pallas kernels, backward(): pl.pallas_call(functools.partial(backward_body, n, part, need, first, len...  324 us
    ppermute x36, waiting for transfers between devices, send(): return lax.ppermute(t, 'dp', pairs)  221 us
    ppermute x36, starting transfers between devices, send(): return lax.ppermute(t, 'dp', pairs)  63 us
    pallas_call x1, Pallas kernels, forward(): pl.pallas_call(functools.partial(forward_body, part), grid=(tokens // til...  61.1 us
    pallas_call x9, Pallas kernels, update(): pl.pallas_call(functools.partial(update_body, len(done), len(after)), gri...  45.4 us
    pallas_call x9, Pallas kernels, place(): pl.pallas_call(functools.partial(place_body, n, pieces, chunk, layer, len...  33.9 us
  transfers between devices with their start and end apart: 45, of which 23 were waited for; matrix products, arithmetic and copies ran while one was open for 2% of the time, Pallas kernels for 47%

profile of v2, /device:TPU:120, one launch (start us, length us, event | category | flops | bytes accessed | tf_op | source)
XLA Modules:
  0.0 786.1 jit_solution(15667417167148836193)
XLA Ops:
  7.3 61.1 %forward.1 = (bf16[4096,512]{1,0:T(8,128)(2,1)}, bf16[4096,512]{1,0:T(8,128)(2,1)}, bf16[4096,512]{1,0:T(8,128)(2,1)}) custom-call(bf16[4096,512]{1,0:T(8,128)(2,1)} %bitcast.54, bf16[2,512,4096]{2,1,0:T(8,128)(2,1)} %refs_3_.23, bf16[2,512,4096]{2,1,0:T(8,128)(2,1)} %refs_4_.23, bf16[2,4096,512]{2,1,0:T(8,128)(2,1)} %refs_5_.25), custom_call_target="tpu_custom_call" | custom-call | flops 51539607552 | bytes 29360128 | tf_op jit(solution)/shard_map/forward/pallas_call | solution.py:52
  68.4 24.0 %backward.9 = (bf16[4,1536,128]{2,1,0:T(8,128)(2,1)}, f32[512,4096]{1,0:T(8,128)}) custom-call(bf16[4096,512]{1,0:T(8,128)(2,1)} %get-tuple-element.112.refs_0_.refs_1_.refs_3_.refs_4_, bf16[4096,512]{1,0:T(8,128)(2,1)} %bitcast.22, bf16[2,512,4096]{2,1,0:T(8,128)(2,1)} %refs_3_.23, bf16[2,512,4096]{2,1,0:T(8,128)(2,1)} %refs_3_.23, ...), custom_call_target="tpu_custom_call" | custom-call | flops 17179869184 | bytes 62914560 | tf_op jit(solution)/shard_map/backward/pallas_call | solution.py:163
  92.6 24.5 %backward.10 = (bf16[4,1536,128]{2,1,0:T(8,128)(2,1)}, f32[512,4096]{1,0:T(8,128)}) custom-call(bf16[4096,512]{1,0:T(8,128)(2,1)} %get-tuple-element.112.refs_0_.refs_1_.refs_3_.refs_4_, bf16[4096,512]{1,0:T(8,128)(2,1)} %bitcast.23, bf16[2,512,4096]{2,1,0:T(8,128)(2,1)} %refs_3_.23, ...), custom_call_target="tpu_custom_call", output_to_operand_aliasing={{1}: (11, {})} | custom-call | flops 17179869184 | bytes 62914560 | tf_op jit(solution)/shard_map/backward/pallas_call | solution.py:163
  117.4 4.1 update.9
  121.5 44.7 %backward.11 = (bf16[4,3072,128]{2,1,0:T(8,128)(2,1)}, f32[512,4096]{1,0:T(8,128)}) custom-call(bf16[4,3,128,128]{3,2,1,0:T(8,128)(2,1)} %get-tuple-element.114.refs_0_.own, bf16[4096,512]{1,0:T(8,128)(2,1)} %get-tuple-element.112.refs_0_.refs_1_.refs_3_.refs_4_, bf16[4096,512]{1,0:T(8,128)(2,1)} %bitcast.24, ...), custom_call_target="tpu_custom_call", output_to_operand_aliasing={{1}: (12, {})} | custom-call | flops 34359738368 | bytes 62914560 | tf_op jit(solution)/shard_map/backward/pallas_call | solution.py:163
  166.3 1.7 collective-permute-start.3
  168.0 1.7 collective-permute-start.2
  169.7 4.2 update.10
  173.9 8.8 %collective-permute-done.3.left = bf16[4,3,128,128]{3,2,1,0:T(8,128)(2,1)S(1)} collective-permute-done((bf16[4,3,128,128]{3,2,1,0:T(8,128)(2,1)S(1)}, bf16[4,3,128,128]{3,2,1,0:T(8,128)(2,1)S(1)}, u32[]{:S(2)}, u32[]{:S(2)}) %collective-permute-start.3) | collective-permute-done | bytes 393248 | tf_op jit(solution)/shard_map/ppermute | solution.py:287
  185.6 44.5 %backward.12 = (bf16[4,3072,128]{2,1,0:T(8,128)(2,1)}, f32[512,4096]{1,0:T(8,128)}) custom-call(bf16[4,3,128,128]{3,2,1,0:T(8,128)(2,1)} %get-tuple-element.132.refs_0_.own, bf16[2,3,128,128]{3,2,1,0:T(8,128)(2,1)} %slice.74.refs_1_, bf16[2,3,128,128]{3,2,1,0:T(8,128)(2,1)} %slice.75.refs_2_, ...), custom_call_target="tpu_custom_call", output_to_operand_aliasing={{1}: (14, {})} | custom-call | flops 34359738368 | bytes 62914560 | tf_op jit(solution)/shard_map/backward/pallas_call | solution.py:163
  231.9 2.5 collective-permute-start.1
  234.5 3.2 collective-permute-start.5
  237.7 9.4 %collective-permute-done.left = bf16[4,3,128,128]{3,2,1,0:T(8,128)(2,1)S(1)} collective-permute-done((bf16[4,3,128,128]{3,2,1,0:T(8,128)(2,1)S(1)}, bf16[4,3,128,128]{3,2,1,0:T(8,128)(2,1)S(1)}, u32[]{:S(2)}, u32[]{:S(2)}) %collective-permute-start) | collective-permute-done | bytes 393248 | tf_op jit(solution)/shard_map/ppermute | solution.py:287
  250.0 3.5 collective-permute-done.4.far_a
  253.5 2.1 collective-permute-done.5.far_b
  256.3 2.9 place.9
  259.2 5.3 update.11
  264.6 46.8 %backward.13 = (bf16[4,3072,128]{2,1,0:T(8,128)(2,1)}, bf16[4096,512]{1,0:T(8,128)(2,1)}) custom-call(bf16[4,3,128,256]{3,2,1,0:T(8,128)(2,1)} %get-tuple-element.131.refs_0_.own, bf16[2,3,128,128]{3,2,1,0:T(8,128)(2,1)} %slice.72.refs_1_, bf16[2,3,128,128]{3,2,1,0:T(8,128)(2,1)} %slice.73.refs_2_, bf16[2,512,4096]{2,1,0:T(8,128)(2,1)} %get-tuple-element.133.refs_3_.refs_0_, ...), custom_call_target="tpu_custom_call" | custom-call | flops 34359738368 | bytes 62914560 | tf_op jit(solution)/shard_map/backward/pallas_call | solution.py:163
  311.9 3.6 collective-permute-start.13
  315.6 3.2 collective-permute-start.8
  320.8 2.9 place.10
  323.8 5.3 update.12
  329.0 14.9 %collective-permute-done.9.left = bf16[4,3,128,256]{3,2,1,0:T(8,128)(2,1)S(1)} collective-permute-done((bf16[4,3,128,256]{3,2,1,0:T(8,128)(2,1)S(1)}, bf16[4,3,128,256]{3,2,1,0:T(8,128)(2,1)S(1)}, u32[]{:S(2)}, u32[]{:S(2)}) %collective-permute-start.9) | collective-permute-done | bytes 786464 | tf_op jit(solution)/shard_map/ppermute | solution.py:287
  346.2 34.9 %backward.15 = bf16[4,3072,128]{2,1,0:T(8,128)(2,1)} custom-call(bf16[4,3,128,256]{3,2,1,0:T(8,128)(2,1)} %get-tuple-element.152.refs_0_.own, bf16[2,3,128,256]{3,2,1,0:T(8,128)(2,1)} %slice.78.refs_1_, bf16[2,3,128,256]{3,2,1,0:T(8,128)(2,1)} %slice.79.refs_2_, bf16[2,512,4096]{2,1,0:T(8,128)(2,1)} %get-tuple-element.155.refs_0_.refs_3_, ...), custom_call_target="tpu_custom_call" | custom-call | flops 25769803776 | bytes 62914560 | tf_op jit(solution)/shard_map/backward/pallas_call | solution.py:163
  381.4 3.8 collective-permute-start.7
  385.2 3.2 collective-permute-start.11
  388.5 14.8 %collective-permute-done.6.left = bf16[4,3,128,256]{3,2,1,0:T(8,128)(2,1)S(1)} collective-permute-done((bf16[4,3,128,256]{3,2,1,0:T(8,128)(2,1)S(1)}, bf16[4,3,128,256]{3,2,1,0:T(8,128)(2,1)S(1)}, u32[]{:S(2)}, u32[]{:S(2)}) %collective-permute-start.6) | collective-permute-done | bytes 786464 | tf_op jit(solution)/shard_map/ppermute | solution.py:287
  404.1 4.4 collective-permute-done.7.right
  409.2 6.6 collective-permute-done.10.far_a
  415.9 6.3 collective-permute-done.11.far_b
  422.9 4.0 place.11
  427.0 5.3 update.13
  432.3 34.9 %backward.14 = bf16[4,3072,128]{2,1,0:T(8,128)(2,1)} custom-call(bf16[4,3,128,256]{3,2,1,0:T(8,128)(2,1)} %get-tuple-element.151.refs_0_.own, bf16[2,3,128,256]{3,2,1,0:T(8,128)(2,1)} %slice.76.refs_1_, bf16[2,3,128,256]{3,2,1,0:T(8,128)(2,1)} %slice.77.refs_2_, bf16[2,512,4096]{2,1,0:T(8,128)(2,1)} %get-tuple-element.158.refs_3_.refs_0_, ...), custom_call_target="tpu_custom_call" | custom-call | flops 25769803776 | bytes 62914560 | tf_op jit(solution)/shard_map/backward/pallas_call | solution.py:163
  467.6 3.8 collective-permute-start.16
  471.4 3.2 collective-permute-start.21
  474.6 32.6 %collective-permute-done.20.far_a = bf16[2,3,128,256]{3,2,1,0:T(8,128)(2,1)S(1)} collective-permute-done((bf16[2,3,128,256]{3,2,1,0:T(8,128)(2,1)S(1)}, bf16[2,3,128,256]{3,2,1,0:T(8,128)(2,1)S(1)}, u32[]{:S(2)}, u32[]{:S(2)}) %collective-permute-start.20) | collective-permute-done | bytes 393248 | tf_op jit(solution)/shard_map/ppermute | solution.py:287
  507.2 7.1 collective-permute-done.21.far_b
  515.1 4.0 place.12
  520.9 5.2 update.14
  526.2 34.9 %backward.17 = bf16[4,3072,128]{2,1,0:T(8,128)(2,1)} custom-call(bf16[4,3,128,256]{3,2,1,0:T(8,128)(2,1)} %get-tuple-element.174.refs_0_.own, bf16[2,3,128,256]{3,2,1,0:T(8,128)(2,1)} %slice.82.refs_1_, bf16[2,3,128,256]{3,2,1,0:T(8,128)(2,1)} %slice.83.refs_2_, bf16[2,512,4096]{2,1,0:T(8,128)(2,1)} %get-tuple-element.177.refs_0_.refs_3_, ...), custom_call_target="tpu_custom_call" | custom-call | flops 25769803776 | bytes 62914560 | tf_op jit(solution)/shard_map/backward/pallas_call | solution.py:163
  561.3 3.8 collective-permute-start.15
  565.1 3.2 collective-permute-start.19
  568.3 34.6 %collective-permute-done.18.far_a = bf16[2,3,128,256]{3,2,1,0:T(8,128)(2,1)S(1)} collective-permute-done((bf16[2,3,128,256]{3,2,1,0:T(8,128)(2,1)S(1)}, bf16[2,3,128,256]{3,2,1,0:T(8,128)(2,1)S(1)}, u32[]{:S(2)}, u32[]{:S(2)}) %collective-permute-start.18) | collective-permute-done | bytes 393248 | tf_op jit(solution)/shard_map/ppermute | solution.py:287
  602.9 7.1 collective-permute-done.19.far_b
  610.8 4.0 place.13
  616.6 5.3 update.15
  621.9 34.9 %backward.16 = bf16[4,3072,128]{2,1,0:T(8,128)(2,1)} custom-call(bf16[4,3,128,256]{3,2,1,0:T(8,128)(2,1)} %get-tuple-element.173.refs_0_.own, bf16[2,3,128,256]{3,2,1,0:T(8,128)(2,1)} %slice.80.refs_1_, bf16[2,3,128,256]{3,2,1,0:T(8,128)(2,1)} %slice.81.refs_2_, bf16[2,512,4096]{2,1,0:T(8,128)(2,1)} %get-tuple-element.180.refs_3_.refs_0_, ...), custom_call_target="tpu_custom_call" | custom-call | flops 25769803776 | bytes 62914560 | tf_op jit(solution)/shard_map/backward/pallas_call | solution.py:163
  656.9 3.7 collective-permute-start.23
  660.6 3.2 collective-permute-start.25
  663.9 27.2 %collective-permute-done.24.far_a = bf16[2,3,128,256]{3,2,1,0:T(8,128)(2,1)S(1)} collective-permute-done((bf16[2,3,128,256]{3,2,1,0:T(8,128)(2,1)S(1)}, bf16[2,3,128,256]{3,2,1,0:T(8,128)(2,1)S(1)}, u32[]{:S(2)}, u32[]{:S(2)}) %collective-permute-start.24) | collective-permute-done | bytes 393248 | tf_op jit(solution)/shard_map/ppermute | solution.py:287
  691.1 5.2 collective-permute-done.25.far_b
  697.1 4.0 place.14
  702.7 5.4 update.16
  708.3 3.8 collective-permute-start.27
  712.0 3.2 collective-permute-start.29
  715.3 23.7 %collective-permute-done.28.far_a = bf16[2,3,128,256]{3,2,1,0:T(8,128)(2,1)S(1)} collective-permute-done((bf16[2,3,128,256]{3,2,1,0:T(8,128)(2,1)S(1)}, bf16[2,3,128,256]{3,2,1,0:T(8,128)(2,1)S(1)}, u32[]{:S(2)}, u32[]{:S(2)}) %collective-permute-start.28) | collective-permute-done | bytes 393248 | tf_op jit(solution)/shard_map/ppermute | solution.py:287
  739.9 4.0 place.15
  745.7 5.4 update.17
  752.4 2.0 collective-permute-start.30
  754.5 3.2 collective-permute-start.35
  757.7 6.9 collective-permute-done.31.left
  764.8 3.3 collective-permute-start.33
  770.3 4.0 place.16
  775.1 4.0 place.17
  (197 shorter events, 32.0 us)
Async XLA Ops:
  7.2 110.2 %reduce-scatter.10.cloned.1.call-start = ((), (), s32[]{:S(2)}) async-start(), calls=%async_computation.9 | async-start | bytes 1966080 | tf_op jit(solution)/shard_map/reduce_scatter | solution.py:321
  92.5 77.2 %reduce-scatter.14.cloned.1.call-start = ((), (), s32[]{:S(2)}) async-start(), calls=%async_computation.11 | async-start | bytes 1966080 | tf_op jit(solution)/shard_map/reduce_scatter | solution.py:321
  117.1 142.2 %reduce-scatter.12.cloned.1.call-start = ((), (), s32[]{:S(2)}) async-start(), calls=%async_computation.10 | async-start | bytes 3932160 | tf_op jit(solution)/shard_map/reduce_scatter | solution.py:321
  121.5 44.8 %copy-start.55 = (bf16[4,3,128,128]{3,2,1,0:T(8,128)(2,1)S(1)}, bf16[4,3,128,128]{3,2,1,0:T(8,128)(2,1)}, u32[]{:S(2)}) copy-start(bf16[4,3,128,128]{3,2,1,0:T(8,128)(2,1)} %get-tuple-element.114.refs_0_.own) | copy-start | bytes 1179652
  166.2 157.5 %reduce-scatter.18.cloned.1.call-start = ((), (), s32[]{:S(2)}) async-start(), calls=%async_computation.13 | async-start | bytes 3932160 | tf_op jit(solution)/shard_map/reduce_scatter | solution.py:321
  166.3 16.4 %collective-permute-start.3 = (bf16[4,3,128,128]{3,2,1,0:T(8,128)(2,1)S(1)}, bf16[4,3,128,128]{3,2,1,0:T(8,128)(2,1)S(1)}, u32[]{:S(2)}, u32[]{:S(2)}) collective-permute-start(bf16[4,3,128,128]{3,2,1,0:T(8,128)(2,1)S(1)} %copy-done.55), channel_id=1, source_target_pairs={{0,1},{1,2},{2,3},{3,0},{4,5},{5,6},{6,7},{7,4},{8,9},{9,10},{10,1... | collective-permute-start | bytes 1179656 | tf_op jit(solution)/shard_map/ppermute | solution.py:287
  168.0 16.8 %collective-permute-start.2 = (bf16[4,3,128,128]{3,2,1,0:T(8,128)(2,1)S(1)}, bf16[4,3,128,128]{3,2,1,0:T(8,128)(2,1)S(1)}, u32[]{:S(2)}, u32[]{:S(2)}) collective-permute-start(bf16[4,3,128,128]{3,2,1,0:T(8,128)(2,1)S(1)} %copy-done.55), channel_id=1, source_target_pairs={{0,3},{1,0},{2,1},{3,2},{4,7},{5,4},{6,5},{7,6},{8,11},{9,8},{10,9... | collective-permute-start | bytes 1179656 | tf_op jit(solution)/shard_map/ppermute | solution.py:287
  182.7 47.3 %copy-start.53 = (bf16[4,3,128,128]{3,2,1,0:T(8,128)(2,1)}, bf16[4,3,128,128]{3,2,1,0:T(8,128)(2,1)S(1)}, u32[]{:S(2)}) copy-start(bf16[4,3,128,128]{3,2,1,0:T(8,128)(2,1)S(1)} %collective-permute-done.3.left) | copy-start | bytes 1179652
  184.8 45.2 %copy-start.54 = (bf16[4,3,128,128]{3,2,1,0:T(8,128)(2,1)}, bf16[4,3,128,128]{3,2,1,0:T(8,128)(2,1)S(1)}, u32[]{:S(2)}) copy-start(bf16[4,3,128,128]{3,2,1,0:T(8,128)(2,1)S(1)} %collective-permute-done.2.right) | copy-start | bytes 1179652
  185.6 45.0 %copy-start.33 = (bf16[4,3,128,128]{3,2,1,0:T(8,128)(2,1)S(1)}, bf16[4,3,128,128]{3,2,1,0:T(8,128)(2,1)}, u32[]{:S(2)}) copy-start(bf16[4,3,128,128]{3,2,1,0:T(8,128)(2,1)} %get-tuple-element.132.refs_0_.own) | copy-start | bytes 1179652
  185.6 48.9 %copy-start.51 = (bf16[2,3,128,128]{3,2,1,0:T(8,128)(2,1)S(1)}, bf16[2,3,128,128]{3,2,1,0:T(8,128)(2,1)}, u32[]{:S(2)}) copy-start(bf16[2,3,128,128]{3,2,1,0:T(8,128)(2,1)} %slice.74.refs_1_) | copy-start | bytes 589828
  185.6 48.9 %copy-start.52 = (bf16[2,3,128,128]{3,2,1,0:T(8,128)(2,1)S(1)}, bf16[2,3,128,128]{3,2,1,0:T(8,128)(2,1)}, u32[]{:S(2)}) copy-start(bf16[2,3,128,128]{3,2,1,0:T(8,128)(2,1)} %slice.75.refs_2_) | copy-start | bytes 589828
  230.1 196.9 %reduce-scatter.16.cloned.1.call-start = ((), (), s32[]{:S(2)}) async-start(), calls=%async_computation.12 | async-start | bytes 3932160 | tf_op jit(solution)/shard_map/reduce_scatter | solution.py:321
  230.6 16.5 %collective-permute-start = (bf16[4,3,128,128]{3,2,1,0:T(8,128)(2,1)S(1)}, bf16[4,3,128,128]{3,2,1,0:T(8,128)(2,1)S(1)}, u32[]{:S(2)}, u32[]{:S(2)}) collective-permute-start(bf16[4,3,128,128]{3,2,1,0:T(8,128)(2,1)S(1)} %copy-done.33), channel_id=1, source_target_pairs={{0,1},{1,2},{2,3},{3,0},{4,5},{5,6},{6,7},{7,4},{8,9},{9,10},{10,1... | collective-permute-start | bytes 1179656 | tf_op jit(solution)/shard_map/ppermute | solution.py:287
  231.9 17.3 %collective-permute-start.1 = (bf16[4,3,128,128]{3,2,1,0:T(8,128)(2,1)S(1)}, bf16[4,3,128,128]{3,2,1,0:T(8,128)(2,1)S(1)}, u32[]{:S(2)}, u32[]{:S(2)}) collective-permute-start(bf16[4,3,128,128]{3,2,1,0:T(8,128)(2,1)S(1)} %copy-done.33), channel_id=1, source_target_pairs={{0,3},{1,0},{2,1},{3,2},{4,7},{5,4},{6,5},{7,6},{8,11},{9,8},{10,9... | collective-permute-start | bytes 1179656 | tf_op jit(solution)/shard_map/ppermute | solution.py:287
  234.4 19.0 %collective-permute-start.4 = (bf16[2,3,128,128]{3,2,1,0:T(8,128)(2,1)S(1)}, bf16[2,3,128,128]{3,2,1,0:T(8,128)(2,1)S(1)}, u32[]{:S(2)}, u32[]{:S(2)}) collective-permute-start(bf16[2,3,128,128]{3,2,1,0:T(8,128)(2,1)S(1)} %copy-done.51), channel_id=1, source_target_pairs={{0,1},{1,2},{2,3},{3,0},{4,5},{5,6},{6,7},{7,4},{8,9},{9,10},{10,1... | collective-permute-start | bytes 589832 | tf_op jit(solution)/shard_map/ppermute | solution.py:287
  234.5 21.1 %collective-permute-start.5 = (bf16[2,3,128,128]{3,2,1,0:T(8,128)(2,1)S(1)}, bf16[2,3,128,128]{3,2,1,0:T(8,128)(2,1)S(1)}, u32[]{:S(2)}, u32[]{:S(2)}) collective-permute-start(bf16[2,3,128,128]{3,2,1,0:T(8,128)(2,1)S(1)} %copy-done.52), channel_id=1, source_target_pairs={{0,3},{1,0},{2,1},{3,2},{4,7},{5,4},{6,5},{7,6},{8,11},{9,8},{10,9... | collective-permute-start | bytes 589832 | tf_op jit(solution)/shard_map/ppermute | solution.py:287
  264.5 47.1 %copy-start.49 = (bf16[2,3,128,128]{3,2,1,0:T(8,128)(2,1)S(1)}, bf16[2,3,128,128]{3,2,1,0:T(8,128)(2,1)}, u32[]{:S(2)}) copy-start(bf16[2,3,128,128]{3,2,1,0:T(8,128)(2,1)} %slice.72.refs_1_) | copy-start | bytes 589828
  264.5 47.4 %copy-start.50 = (bf16[2,3,128,128]{3,2,1,0:T(8,128)(2,1)S(1)}, bf16[2,3,128,128]{3,2,1,0:T(8,128)(2,1)}, u32[]{:S(2)}) copy-start(bf16[2,3,128,128]{3,2,1,0:T(8,128)(2,1)} %slice.73.refs_2_) | copy-start | bytes 589828
  264.6 51.0 %copy-start.32 = (bf16[4,3,128,256]{3,2,1,0:T(8,128)(2,1)S(1)}, bf16[4,3,128,256]{3,2,1,0:T(8,128)(2,1)}, u32[]{:S(2)}) copy-start(bf16[4,3,128,256]{3,2,1,0:T(8,128)(2,1)} %get-tuple-element.131.refs_0_.own) | copy-start | bytes 2359300
  311.4 209.5 %reduce-scatter.22.cloned.1.call-start = ((), (), s32[]{:S(2)}) async-start(), calls=%async_computation.15 | async-start | bytes 3932160 | tf_op jit(solution)/shard_map/reduce_scatter | solution.py:321
  311.7 7.4 collective-permute-start.12
  311.9 8.2 %collective-permute-start.13 = (bf16[2,3,128,128]{3,2,1,0:T(8,128)(2,1)S(1)}, bf16[2,3,128,128]{3,2,1,0:T(8,128)(2,1)S(1)}, u32[]{:S(2)}, u32[]{:S(2)}) collective-permute-start(bf16[2,3,128,128]{3,2,1,0:T(8,128)(2,1)S(1)} %copy-done.50), channel_id=1, source_target_pairs={{0,3},{1,0},{2,1},{3,2},{4,7},{5,4},{6,5},{7,6},{8,11},{9,8},{10,9... | collective-permute-start | bytes 589832 | tf_op jit(solution)/shard_map/ppermute | solution.py:287
  315.6 28.3 %collective-permute-start.9 = (bf16[4,3,128,256]{3,2,1,0:T(8,128)(2,1)S(1)}, bf16[4,3,128,256]{3,2,1,0:T(8,128)(2,1)S(1)}, u32[]{:S(2)}, u32[]{:S(2)}) collective-permute-start(bf16[4,3,128,256]{3,2,1,0:T(8,128)(2,1)S(1)} %copy-done.32), channel_id=1, source_target_pairs={{0,1},{1,2},{2,3},{3,0},{4,5},{5,6},{6,7},{7,4},{8,9},{9,10},{10,1... | collective-permute-start | bytes 2359304 | tf_op jit(solution)/shard_map/ppermute | solution.py:287
  315.6 29.9 %collective-permute-start.8 = (bf16[4,3,128,256]{3,2,1,0:T(8,128)(2,1)S(1)}, bf16[4,3,128,256]{3,2,1,0:T(8,128)(2,1)S(1)}, u32[]{:S(2)}, u32[]{:S(2)}) collective-permute-start(bf16[4,3,128,256]{3,2,1,0:T(8,128)(2,1)S(1)} %copy-done.32), channel_id=1, source_target_pairs={{0,3},{1,0},{2,1},{3,2},{4,7},{5,4},{6,5},{7,6},{8,11},{9,8},{10,9... | collective-permute-start | bytes 2359304 | tf_op jit(solution)/shard_map/ppermute | solution.py:287
  343.9 37.2 %copy-start.5 = (bf16[4,3,128,256]{3,2,1,0:T(8,128)(2,1)}, bf16[4,3,128,256]{3,2,1,0:T(8,128)(2,1)S(1)}, u32[]{:S(2)}) copy-start(bf16[4,3,128,256]{3,2,1,0:T(8,128)(2,1)S(1)} %collective-permute-done.9.left) | copy-start | bytes 2359300
  345.4 35.7 %copy-start.10 = (bf16[4,3,128,256]{3,2,1,0:T(8,128)(2,1)}, bf16[4,3,128,256]{3,2,1,0:T(8,128)(2,1)S(1)}, u32[]{:S(2)}) copy-start(bf16[4,3,128,256]{3,2,1,0:T(8,128)(2,1)S(1)} %collective-permute-done.8.right) | copy-start | bytes 2359300
  346.2 39.0 %copy-start.26 = (bf16[2,3,128,256]{3,2,1,0:T(8,128)(2,1)S(1)}, bf16[2,3,128,256]{3,2,1,0:T(8,128)(2,1)}, u32[]{:S(2)}) copy-start(bf16[2,3,128,256]{3,2,1,0:T(8,128)(2,1)} %slice.78.refs_1_) | copy-start | bytes 1179652
  346.2 39.0 %copy-start.27 = (bf16[2,3,128,256]{3,2,1,0:T(8,128)(2,1)S(1)}, bf16[2,3,128,256]{3,2,1,0:T(8,128)(2,1)}, u32[]{:S(2)}) copy-start(bf16[2,3,128,256]{3,2,1,0:T(8,128)(2,1)} %slice.79.refs_2_) | copy-start | bytes 1179652
  381.2 235.4 %reduce-scatter.20.cloned.1.call-start = ((), (), s32[]{:S(2)}) async-start(), calls=%async_computation.14 | async-start | bytes 3932160 | tf_op jit(solution)/shard_map/reduce_scatter | solution.py:321
  381.3 21.9 %collective-permute-start.6 = (bf16[4,3,128,256]{3,2,1,0:T(8,128)(2,1)S(1)}, bf16[4,3,128,256]{3,2,1,0:T(8,128)(2,1)S(1)}, u32[]{:S(2)}, u32[]{:S(2)}) collective-permute-start(bf16[4,3,128,256]{3,2,1,0:T(8,128)(2,1)S(1)} %copy-done), channel_id=1, source_target_pairs={{0,1},{1,2},{2,3},{3,0},{4,5},{5,6},{6,7},{7,4},{8,9},{9,10},{10,1... | collective-permute-start | bytes 2359304 | tf_op jit(solution)/shard_map/ppermute | solution.py:287
  381.4 27.0 %collective-permute-start.7 = (bf16[4,3,128,256]{3,2,1,0:T(8,128)(2,1)S(1)}, bf16[4,3,128,256]{3,2,1,0:T(8,128)(2,1)S(1)}, u32[]{:S(2)}, u32[]{:S(2)}) collective-permute-start(bf16[4,3,128,256]{3,2,1,0:T(8,128)(2,1)S(1)} %copy-done), channel_id=1, source_target_pairs={{0,3},{1,0},{2,1},{3,2},{4,7},{5,4},{6,5},{7,6},{8,11},{9,8},{10,9... | collective-permute-start | bytes 2359304 | tf_op jit(solution)/shard_map/ppermute | solution.py:287
  385.2 30.6 %collective-permute-start.10 = (bf16[2,3,128,256]{3,2,1,0:T(8,128)(2,1)S(1)}, bf16[2,3,128,256]{3,2,1,0:T(8,128)(2,1)S(1)}, u32[]{:S(2)}, u32[]{:S(2)}) collective-permute-start(bf16[2,3,128,256]{3,2,1,0:T(8,128)(2,1)S(1)} %copy-done.26), channel_id=1, source_target_pairs={{0,1},{1,2},{2,3},{3,0},{4,5},{5,6},{6,7},{7,4},{8,9},{9,10},{10,1... | collective-permute-start | bytes 1179656 | tf_op jit(solution)/shard_map/ppermute | solution.py:287
  385.2 36.9 %collective-permute-start.11 = (bf16[2,3,128,256]{3,2,1,0:T(8,128)(2,1)S(1)}, bf16[2,3,128,256]{3,2,1,0:T(8,128)(2,1)S(1)}, u32[]{:S(2)}, u32[]{:S(2)}) collective-permute-start(bf16[2,3,128,256]{3,2,1,0:T(8,128)(2,1)S(1)} %copy-done.27), channel_id=1, source_target_pairs={{0,3},{1,0},{2,1},{3,2},{4,7},{5,4},{6,5},{7,6},{8,11},{9,8},{10,9... | collective-permute-start | bytes 1179656 | tf_op jit(solution)/shard_map/ppermute | solution.py:287
  432.3 39.1 %copy-start.18 = (bf16[2,3,128,256]{3,2,1,0:T(8,128)(2,1)S(1)}, bf16[2,3,128,256]{3,2,1,0:T(8,128)(2,1)}, u32[]{:S(2)}) copy-start(bf16[2,3,128,256]{3,2,1,0:T(8,128)(2,1)} %slice.76.refs_1_) | copy-start | bytes 1179652
  432.3 39.1 %copy-start.19 = (bf16[2,3,128,256]{3,2,1,0:T(8,128)(2,1)S(1)}, bf16[2,3,128,256]{3,2,1,0:T(8,128)(2,1)}, u32[]{:S(2)}) copy-start(bf16[2,3,128,256]{3,2,1,0:T(8,128)(2,1)} %slice.77.refs_2_) | copy-start | bytes 1179652
  467.2 235.5 %reduce-scatter.26.cloned.1.call-start = ((), (), s32[]{:S(2)}) async-start(), calls=%async_computation.17 | async-start | bytes 3932160 | tf_op jit(solution)/shard_map/reduce_scatter | solution.py:321
  467.5 51.6 %collective-permute-start.17 = (bf16[4,3,128,256]{3,2,1,0:T(8,128)(2,1)S(1)}, bf16[4,3,128,256]{3,2,1,0:T(8,128)(2,1)S(1)}, u32[]{:S(2)}, u32[]{:S(2)}) collective-permute-start(bf16[4,3,128,256]{3,2,1,0:T(8,128)(2,1)S(1)} %copy-done.1), channel_id=1, source_target_pairs={{0,1},{1,2},{2,3},{3,0},{4,5},{5,6},{6,7},{7,4},{8,9},{9,10},{10,1... | collective-permute-start | bytes 2359304 | tf_op jit(solution)/shard_map/ppermute | solution.py:287
  467.6 52.4 %collective-permute-start.16 = (bf16[4,3,128,256]{3,2,1,0:T(8,128)(2,1)S(1)}, bf16[4,3,128,256]{3,2,1,0:T(8,128)(2,1)S(1)}, u32[]{:S(2)}, u32[]{:S(2)}) collective-permute-start(bf16[4,3,128,256]{3,2,1,0:T(8,128)(2,1)S(1)} %copy-done.1), channel_id=1, source_target_pairs={{0,3},{1,0},{2,1},{3,2},{4,7},{5,4},{6,5},{7,6},{8,11},{9,8},{10,9... | collective-permute-start | bytes 2359304 | tf_op jit(solution)/shard_map/ppermute | solution.py:287
  471.4 35.8 %collective-permute-start.20 = (bf16[2,3,128,256]{3,2,1,0:T(8,128)(2,1)S(1)}, bf16[2,3,128,256]{3,2,1,0:T(8,128)(2,1)S(1)}, u32[]{:S(2)}, u32[]{:S(2)}) collective-permute-start(bf16[2,3,128,256]{3,2,1,0:T(8,128)(2,1)S(1)} %copy-done.18), channel_id=1, source_target_pairs={{0,1},{1,2},{2,3},{3,0},{4,5},{5,6},{6,7},{7,4},{8,9},{9,10},{10,1... | collective-permute-start | bytes 1179656 | tf_op jit(solution)/shard_map/ppermute | solution.py:287
  471.4 43.0 %collective-permute-start.21 = (bf16[2,3,128,256]{3,2,1,0:T(8,128)(2,1)S(1)}, bf16[2,3,128,256]{3,2,1,0:T(8,128)(2,1)S(1)}, u32[]{:S(2)}, u32[]{:S(2)}) collective-permute-start(bf16[2,3,128,256]{3,2,1,0:T(8,128)(2,1)S(1)} %copy-done.19), channel_id=1, source_target_pairs={{0,3},{1,0},{2,1},{3,2},{4,7},{5,4},{6,5},{7,6},{8,11},{9,8},{10,9... | collective-permute-start | bytes 1179656 | tf_op jit(solution)/shard_map/ppermute | solution.py:287
  526.1 39.0 %copy-start.22 = (bf16[2,3,128,256]{3,2,1,0:T(8,128)(2,1)S(1)}, bf16[2,3,128,256]{3,2,1,0:T(8,128)(2,1)}, u32[]{:S(2)}) copy-start(bf16[2,3,128,256]{3,2,1,0:T(8,128)(2,1)} %slice.82.refs_1_) | copy-start | bytes 1179652
  526.2 39.0 %copy-start.23 = (bf16[2,3,128,256]{3,2,1,0:T(8,128)(2,1)S(1)}, bf16[2,3,128,256]{3,2,1,0:T(8,128)(2,1)}, u32[]{:S(2)}) copy-start(bf16[2,3,128,256]{3,2,1,0:T(8,128)(2,1)} %slice.83.refs_2_) | copy-start | bytes 1179652
  561.1 184.6 %reduce-scatter.24.cloned.1.call-start = ((), (), s32[]{:S(2)}) async-start(), calls=%async_computation.16 | async-start | bytes 3932160 | tf_op jit(solution)/shard_map/reduce_scatter | solution.py:321
  561.2 53.6 %collective-permute-start.14 = (bf16[4,3,128,256]{3,2,1,0:T(8,128)(2,1)S(1)}, bf16[4,3,128,256]{3,2,1,0:T(8,128)(2,1)S(1)}, u32[]{:S(2)}, u32[]{:S(2)}) collective-permute-start(bf16[4,3,128,256]{3,2,1,0:T(8,128)(2,1)S(1)} %copy-done.2), channel_id=1, source_target_pairs={{0,1},{1,2},{2,3},{3,0},{4,5},{5,6},{6,7},{7,4},{8,9},{9,10},{10,1... | collective-permute-start | bytes 2359304 | tf_op jit(solution)/shard_map/ppermute | solution.py:287
  561.3 54.4 %collective-permute-start.15 = (bf16[4,3,128,256]{3,2,1,0:T(8,128)(2,1)S(1)}, bf16[4,3,128,256]{3,2,1,0:T(8,128)(2,1)S(1)}, u32[]{:S(2)}, u32[]{:S(2)}) collective-permute-start(bf16[4,3,128,256]{3,2,1,0:T(8,128)(2,1)S(1)} %copy-done.2), channel_id=1, source_target_pairs={{0,3},{1,0},{2,1},{3,2},{4,7},{5,4},{6,5},{7,6},{8,11},{9,8},{10,9... | collective-permute-start | bytes 2359304 | tf_op jit(solution)/shard_map/ppermute | solution.py:287
  565.1 37.8 %collective-permute-start.18 = (bf16[2,3,128,256]{3,2,1,0:T(8,128)(2,1)S(1)}, bf16[2,3,128,256]{3,2,1,0:T(8,128)(2,1)S(1)}, u32[]{:S(2)}, u32[]{:S(2)}) collective-permute-start(bf16[2,3,128,256]{3,2,1,0:T(8,128)(2,1)S(1)} %copy-done.22), channel_id=1, source_target_pairs={{0,1},{1,2},{2,3},{3,0},{4,5},{5,6},{6,7},{7,4},{8,9},{9,10},{10,1... | collective-permute-start | bytes 1179656 | tf_op jit(solution)/shard_map/ppermute | solution.py:287
  565.1 44.9 %collective-permute-start.19 = (bf16[2,3,128,256]{3,2,1,0:T(8,128)(2,1)S(1)}, bf16[2,3,128,256]{3,2,1,0:T(8,128)(2,1)S(1)}, u32[]{:S(2)}, u32[]{:S(2)}) collective-permute-start(bf16[2,3,128,256]{3,2,1,0:T(8,128)(2,1)S(1)} %copy-done.23), channel_id=1, source_target_pairs={{0,3},{1,0},{2,1},{3,2},{4,7},{5,4},{6,5},{7,6},{8,11},{9,8},{10,9... | collective-permute-start | bytes 1179656 | tf_op jit(solution)/shard_map/ppermute | solution.py:287
  621.9 38.8 %copy-start.24 = (bf16[2,3,128,256]{3,2,1,0:T(8,128)(2,1)S(1)}, bf16[2,3,128,256]{3,2,1,0:T(8,128)(2,1)}, u32[]{:S(2)}) copy-start(bf16[2,3,128,256]{3,2,1,0:T(8,128)(2,1)} %slice.80.refs_1_) | copy-start | bytes 1179652
  621.9 38.8 %copy-start.25 = (bf16[2,3,128,256]{3,2,1,0:T(8,128)(2,1)S(1)}, bf16[2,3,128,256]{3,2,1,0:T(8,128)(2,1)}, u32[]{:S(2)}) copy-start(bf16[2,3,128,256]{3,2,1,0:T(8,128)(2,1)} %slice.81.refs_2_) | copy-start | bytes 1179652
  656.8 44.3 %collective-permute-start.22 = (bf16[4,3,128,256]{3,2,1,0:T(8,128)(2,1)S(1)}, bf16[4,3,128,256]{3,2,1,0:T(8,128)(2,1)S(1)}, u32[]{:S(2)}, u32[]{:S(2)}) collective-permute-start(bf16[4,3,128,256]{3,2,1,0:T(8,128)(2,1)S(1)} %copy-done.3), channel_id=1, source_target_pairs={{0,1},{1,2},{2,3},{3,0},{4,5},{5,6},{6,7},{7,4},{8,9},{9,10},{10,1... | collective-permute-start | bytes 2359304 | tf_op jit(solution)/shard_map/ppermute | solution.py:287
  656.9 45.0 %collective-permute-start.23 = (bf16[4,3,128,256]{3,2,1,0:T(8,128)(2,1)S(1)}, bf16[4,3,128,256]{3,2,1,0:T(8,128)(2,1)S(1)}, u32[]{:S(2)}, u32[]{:S(2)}) collective-permute-start(bf16[4,3,128,256]{3,2,1,0:T(8,128)(2,1)S(1)} %copy-done.3), channel_id=1, source_target_pairs={{0,3},{1,0},{2,1},{3,2},{4,7},{5,4},{6,5},{7,6},{8,11},{9,8},{10,9... | collective-permute-start | bytes 2359304 | tf_op jit(solution)/shard_map/ppermute | solution.py:287
  660.6 30.5 %collective-permute-start.24 = (bf16[2,3,128,256]{3,2,1,0:T(8,128)(2,1)S(1)}, bf16[2,3,128,256]{3,2,1,0:T(8,128)(2,1)S(1)}, u32[]{:S(2)}, u32[]{:S(2)}) collective-permute-start(bf16[2,3,128,256]{3,2,1,0:T(8,128)(2,1)S(1)} %copy-done.24), channel_id=1, source_target_pairs={{0,1},{1,2},{2,3},{3,0},{4,5},{5,6},{6,7},{7,4},{8,9},{9,10},{10,1... | collective-permute-start | bytes 1179656 | tf_op jit(solution)/shard_map/ppermute | solution.py:287
  660.6 35.7 %collective-permute-start.25 = (bf16[2,3,128,256]{3,2,1,0:T(8,128)(2,1)S(1)}, bf16[2,3,128,256]{3,2,1,0:T(8,128)(2,1)S(1)}, u32[]{:S(2)}, u32[]{:S(2)}) collective-permute-start(bf16[2,3,128,256]{3,2,1,0:T(8,128)(2,1)S(1)} %copy-done.25), channel_id=1, source_target_pairs={{0,3},{1,0},{2,1},{3,2},{4,7},{5,4},{6,5},{7,6},{8,11},{9,8},{10,9... | collective-permute-start | bytes 1179656 | tf_op jit(solution)/shard_map/ppermute | solution.py:287
  708.2 35.8 %collective-permute-start.26 = (bf16[4,3,128,256]{3,2,1,0:T(8,128)(2,1)}, bf16[4,3,128,256]{3,2,1,0:T(8,128)(2,1)S(1)}, u32[]{:S(2)}, u32[]{:S(2)}) collective-permute-start(bf16[4,3,128,256]{3,2,1,0:T(8,128)(2,1)} %get-tuple-element.196.own), channel_id=1, source_target_pairs={{0,1},{1,2},{2,3},{3,0},{4,5},{5,6},{6,7},{7,4},{8,9},{9,10},{10,1... | collective-permute-start | bytes 2359304 | tf_op jit(solution)/shard_map/ppermute | solution.py:287
  708.3 36.6 %collective-permute-start.27 = (bf16[4,3,128,256]{3,2,1,0:T(8,128)(2,1)}, bf16[4,3,128,256]{3,2,1,0:T(8,128)(2,1)S(1)}, u32[]{:S(2)}, u32[]{:S(2)}) collective-permute-start(bf16[4,3,128,256]{3,2,1,0:T(8,128)(2,1)} %get-tuple-element.196.own), channel_id=1, source_target_pairs={{0,3},{1,0},{2,1},{3,2},{4,7},{5,4},{6,5},{7,6},{8,11},{9,8},{10,9... | collective-permute-start | bytes 2359304 | tf_op jit(solution)/shard_map/ppermute | solution.py:287
  712.0 26.9 %collective-permute-start.28 = (bf16[2,3,128,256]{3,2,1,0:T(8,128)(2,1)S(1)}, bf16[2,3,128,256]{3,2,1,0:T(8,128)(2,1)S(1)}, u32[]{:S(2)}, u32[]{:S(2)}) collective-permute-start(bf16[2,3,128,256]{3,2,1,0:T(8,128)(2,1)S(1)} %copy-done.28), channel_id=1, source_target_pairs={{0,1},{1,2},{2,3},{3,0},{4,5},{5,6},{6,7},{7,4},{8,9},{9,10},{10,1... | collective-permute-start | bytes 1179656 | tf_op jit(solution)/shard_map/ppermute | solution.py:287
  712.0 26.9 %collective-permute-start.29 = (bf16[2,3,128,256]{3,2,1,0:T(8,128)(2,1)S(1)}, bf16[2,3,128,256]{3,2,1,0:T(8,128)(2,1)S(1)}, u32[]{:S(2)}, u32[]{:S(2)}) collective-permute-start(bf16[2,3,128,256]{3,2,1,0:T(8,128)(2,1)S(1)} %copy-done.29), channel_id=1, source_target_pairs={{0,3},{1,0},{2,1},{3,2},{4,7},{5,4},{6,5},{7,6},{8,11},{9,8},{10,9... | collective-permute-start | bytes 1179656 | tf_op jit(solution)/shard_map/ppermute | solution.py:287
  751.1 13.5 %collective-permute-start.31 = (bf16[4,3,128,256]{3,2,1,0:T(8,128)(2,1)}, bf16[4,3,128,256]{3,2,1,0:T(8,128)(2,1)S(1)}, u32[]{:S(2)}, u32[]{:S(2)}) collective-permute-start(bf16[4,3,128,256]{3,2,1,0:T(8,128)(2,1)} %get-tuple-element.200.own), channel_id=1, source_target_pairs={{0,1},{1,2},{2,3},{3,0},{4,5},{5,6},{6,7},{7,4},{8,9},{9,10},{10,1... | collective-permute-start | bytes 2359304 | tf_op jit(solution)/shard_map/ppermute | solution.py:287
  752.4 12.3 %collective-permute-start.30 = (bf16[4,3,128,256]{3,2,1,0:T(8,128)(2,1)}, bf16[4,3,128,256]{3,2,1,0:T(8,128)(2,1)S(1)}, u32[]{:S(2)}, u32[]{:S(2)}) collective-permute-start(bf16[4,3,128,256]{3,2,1,0:T(8,128)(2,1)} %get-tuple-element.200.own), channel_id=1, source_target_pairs={{0,3},{1,0},{2,1},{3,2},{4,7},{5,4},{6,5},{7,6},{8,11},{9,8},{10,9... | collective-permute-start | bytes 2359304 | tf_op jit(solution)/shard_map/ppermute | solution.py:287
  754.4 14.4 %collective-permute-start.34 = (bf16[2,3,128,256]{3,2,1,0:T(8,128)(2,1)S(1)}, bf16[2,3,128,256]{3,2,1,0:T(8,128)(2,1)S(1)}, u32[]{:S(2)}, u32[]{:S(2)}) collective-permute-start(bf16[2,3,128,256]{3,2,1,0:T(8,128)(2,1)S(1)} %copy-done.20), channel_id=1, source_target_pairs={{0,1},{1,2},{2,3},{3,0},{4,5},{5,6},{6,7},{7,4},{8,9},{9,10},{10,1... | collective-permute-start | bytes 1179656 | tf_op jit(solution)/shard_map/ppermute | solution.py:287
  754.5 14.4 %collective-permute-start.35 = (bf16[2,3,128,256]{3,2,1,0:T(8,128)(2,1)S(1)}, bf16[2,3,128,256]{3,2,1,0:T(8,128)(2,1)S(1)}, u32[]{:S(2)}, u32[]{:S(2)}) collective-permute-start(bf16[2,3,128,256]{3,2,1,0:T(8,128)(2,1)S(1)} %copy-done.21), channel_id=1, source_target_pairs={{0,3},{1,0},{2,1},{3,2},{4,7},{5,4},{6,5},{7,6},{8,11},{9,8},{10,9... | collective-permute-start | bytes 1179656 | tf_op jit(solution)/shard_map/ppermute | solution.py:287
  764.6 9.7 %collective-permute-start.32 = (bf16[2,3,128,256]{3,2,1,0:T(8,128)(2,1)S(1)}, bf16[2,3,128,256]{3,2,1,0:T(8,128)(2,1)S(1)}, u32[]{:S(2)}, u32[]{:S(2)}) collective-permute-start(bf16[2,3,128,256]{3,2,1,0:T(8,128)(2,1)S(1)} %slice.88), channel_id=1, source_target_pairs={{0,1},{1,2},{2,3},{3,0},{4,5},{5,6},{6,7},{7,4},{8,9},{9,10},{10,1... | collective-permute-start | bytes 1179656 | tf_op jit(solution)/shard_map/ppermute | solution.py:287
  764.8 9.6 %collective-permute-start.33 = (bf16[2,3,128,256]{3,2,1,0:T(8,128)(2,1)S(1)}, bf16[2,3,128,256]{3,2,1,0:T(8,128)(2,1)}, u32[]{:S(2)}, u32[]{:S(2)}) collective-permute-start(bf16[2,3,128,256]{3,2,1,0:T(8,128)(2,1)S(1)} %slice.89), channel_id=1, source_target_pairs={{0,3},{1,0},{2,1},{3,2},{4,7},{5,4},{6,5},{7,6},{8,11},{9,8},{10,9... | collective-permute-start | bytes 1179656 | tf_op jit(solution)/shard_map/ppermute | solution.py:287
  (39 other events, 353.2 us)
Sparse Core Ops, SparseCore 0:
  92.6 23.1 reduce-scatter.9
  118.6 21.7 reduce-scatter.13
  166.4 38.9 reduce-scatter.11
  230.3 41.0 reduce-scatter.17
  311.6 43.7 reduce-scatter.15
  381.3 47.6 reduce-scatter.21
  467.4 53.6 reduce-scatter.19
  561.2 56.0 reduce-scatter.25
  656.9 44.3 reduce-scatter.23
